TPU v7x, 32 devices: a whole 2x2x4 slice. The times are simulated.
32 devices in a mesh: node: 8 (over z, x), dev: 4 (over y, core).
Axes of the slice: x: 2, y: 2, z: 4, core: 2. Of those that a mesh axis runs over, the one named last changes fastest.
Arguments:
- kv_pages: bfloat16 [4096, 1, 2, 16, 1024], P(('node', 'dev')), may hold values from -6 to 6
- new_slot: int32 [4096], P(('node', 'dev')), may hold values from 0 to 4095, as said below
- request_rate: float32 [512], P(('node', 'dev')), may hold values from 0.25 to 4
- page_table: int32 [512, 128], P(('node', 'dev')), may hold values from 0 to 4095
Outputs:
- migrated: bfloat16 [4096, 1, 2, 16, 1024], P(('node', 'dev'))
- device_load: float32 [32], replicated
Inputs may be any that keep to these rules, and one draw needn't show every extreme that they name: new_slot is a permutation of the slots; slot p lies on device p // 128. Every device sends exactly 31 of its pages to other devices, at most one to any one device, and receives exactly 31 into the slots that its leaving pages free; its other pages keep their slots.
All inputs are finite; a program needn't handle non-finite values.
Results may differ from a plain program's by a relative error of at most 0.001.
Values may be sent and summed in bfloat16 or wider, within the bound.
No kernel may reach another device: no remote copies, remote signals or barrier semaphores. Data moves between devices by JAX's collectives and lax.ppermute only.
A program may use at most 128 MiB of HBM per device.

v0:
```python
import jax
import jax.numpy as jnp
from jax import lax
from jax.sharding import PartitionSpec as P


def on_device(kv_pages, new_slot, request_rate, page_table):
    page_dev = kv_pages.shape[0]
    devices = lax.axis_size(("node", "dev"))
    myself = lax.axis_index(("node", "dev"))
    owners = new_slot // page_dev
    local_ids = jnp.arange(page_dev, dtype=jnp.int32)
    targets = jnp.arange(devices, dtype=jnp.int32)
    flat_pages = kv_pages.reshape(page_dev, -1)
    leaving = owners != myself
    matches = owners[:, None] == targets[None, :]
    sending = jnp.logical_and(matches, leaving[:, None])
    pack_sel = sending.T.astype(jnp.bfloat16)
    outgoing = jnp.dot(pack_sel, flat_pages, preferred_element_type=jnp.float32).astype(
        jnp.bfloat16
    )
    outgoing = outgoing.reshape((devices,) + kv_pages.shape[1:])
    local_target = new_slot % page_dev
    dest_local = jnp.sum(jnp.where(sending, local_target[:, None], 0), axis=0)
    filled = jnp.any(sending, axis=0)
    dest_local = jnp.where(filled, dest_local, page_dev)
    arrived, arrived_slot = (
        lax.all_to_all(outgoing, ("node", "dev"), split_axis=0, concat_axis=0, tiled=True),
        lax.all_to_all(dest_local, ("node", "dev"), split_axis=0, concat_axis=0, tiled=True),
    )
    weights = jnp.broadcast_to(request_rate[:, None], page_table.shape).reshape(-1)
    heat_local = (
        jnp.zeros((devices * page_dev,), jnp.float32).at[page_table.reshape(-1)].add(weights)
    )
    heat_own = lax.psum_scatter(heat_local, ("node", "dev"), scatter_dimension=0, tiled=True)
    owner_terms = jnp.sum(jnp.where(matches, heat_own[:, None], 0.0), axis=0)
    summed = lax.psum(owner_terms, ("node", "dev"))
    device_load = summed / (page_table.shape[1] * page_table.shape[0])
    place_hit = arrived_slot[None, :] == local_ids[:, None]
    place_sel = place_hit.astype(jnp.bfloat16)
    received = jnp.dot(
        place_sel, arrived.reshape(devices, -1), preferred_element_type=jnp.float32
    ).astype(jnp.bfloat16)
    arrival = jnp.any(place_hit, axis=1)
    migrated = jnp.where(arrival[:, None], received, flat_pages).reshape(kv_pages.shape)
    return (migrated, device_load)


def solution(mesh):
    in_specs = (
        P(("node", "dev"), None, None, None, None),
        P(("node", "dev")),
        P(("node", "dev")),
        P(("node", "dev"), None),
    )
    out_specs = (P(("node", "dev"), None, None, None, None), P())
    return jax.shard_map(
        on_device, mesh=mesh, in_specs=in_specs, out_specs=out_specs, check_vma=False
    )
```

profile of v0, /device:TPU:14, one launch (start us, length us, event | category | flops | bytes accessed | tf_op | source)
XLA Modules:
  0.0 167.9 jit_solution(4740667788350288696)
XLA Ops:
  0.6 0.0 copy-start
  0.6 0.7 and_select_fusion
  1.3 0.7 broadcast_compare_fusion
  2.0 0.1 fusion.4
  2.1 0.1 select_reduce_fusion.1
  2.2 0.7 copy.13
  2.9 6.0 %all-to-all-start = ((s32[32,1,1]{2,1,0:T(1,128)}), s32[32,1,1]{2,1,0:T(1,128)S(1)}, u32[]{:S(2)}, u32[]{:S(2)}) async-start(s32[32,1,1]{2,1,0:T(1,128)} %copy.13), calls=%async_computation | async-start | bytes 32768 | tf_op jit(solution)/shard_map/all_to_all | solution.py:29
  8.9 12.8 %copy.16 = bf16[16,8,32,1024]{3,1,2,0:T(8,128)(2,1)} copy(bf16[16,8,32,1024]{3,2,1,0:T(8,128)(2,1)} %bitcast.30) | data formatting | bytes 16777216
  21.7 4.6 %convolution_convert_fusion.1 = bf16[32,32768]{1,0:T(8,128)(2,1)S(1)} fusion(bf16[128,32768]{1,0:T(8,128)(2,1)} %bitcast.26, s32[128]{0:T(128)S(1)} %get-tuple-element.11, pred[128]{0:T(512)(128)(4,1)S(1)} %get-tuple-element.10), kind=kOutput, calls=%fused_computation.3 | convolution fusion | flops 269492224 | bytes 10486400 | tf_op jit(solution)/shard_map/dot_general | solution.py:19
  26.3 2.5 %copy.17 = bf16[4,8,32,1024]{3,2,1,0:T(8,128)(2,1)} copy(bf16[4,8,32,1024]{3,1,2,0:T(8,128)(2,1)S(1)} %bitcast.33) | data formatting | bytes 4194304
  28.8 0.0 all-to-all-done
  28.8 5.8 %all-to-all-start.1 = ((bf16[32,1,2,16,1024]{4,3,2,1,0:T(8,128)(2,1)}), bf16[32,1,2,16,1024]{4,3,2,1,0:T(8,128)(2,1)S(1)}, u32[]{:S(2)}, u32[]{:S(2)}) async-start(bf16[32,1,2,16,1024]{4,3,2,1,0:T(8,128)(2,1)} %bitcast.1), calls=%async_computation.1 | async-start | bytes 4194304 | tf_op jit(solution)/shard_map/all_to_all | solution.py:28
  34.7 0.1 broadcast_bitcast_fusion
  34.8 11.2 %scatter_custom_fusion = f32[4096]{0:T(1024)S(1)} fusion(s32[2048]{0:T(1024)S(1)} %bitcast.35, f32[2048]{0:T(1024)S(1)} %broadcast_bitcast_fusion, f32[]{:T(128)} %constant.48.clone.1), kind=kCustom, calls=%fused_computation.12 | custom fusion | flops 2048 | bytes 16388 | tf_op jit(solution)/shard_map/scatter-add | solution.py:33
  46.0 55.7 %all-reduce = f32[4096]{0:T(1024)S(1)} all-reduce(f32[4096]{0:T(1024)S(1)} %scatter_custom_fusion), channel_id=2, replica_groups=mesh['node'=8,'dev'=4] {'node','dev'}, use_global_device_ids=true, to_apply=%region_4.5.clone | all-reduce | flops 4096 | bytes 32768
  101.7 0.1 dynamic-slice
  101.8 0.1 select_reduce_fusion
  101.9 42.0 %psum.7 = f32[32]{0:T(128)S(1)} all-reduce(f32[32]{0:T(128)S(1)} %select_reduce_fusion), channel_id=1, replica_groups=mesh['node'=8,'dev'=4] {'node','dev'}, use_global_device_ids=true, to_apply=%region_6.7 | all-reduce | flops 32 | bytes 256 | tf_op jit(solution)/shard_map/psum | solution.py:37
  144.0 0.5 broadcast_multiply_fusion
  144.5 0.7 reduce
  145.1 0.1 fusion.1
  145.2 1.2 copy.18
  146.4 9.1 %fusion = bf16[128,32768]{1,0:T(8,128)(2,1)} fusion(bf16[128,32768]{1,0:T(8,128)(2,1)} %bitcast.27, bf16[32,32768]{1,0:T(8,128)(2,1)S(1)} %bitcast.29, pred[128]{0:T(512)(128)(4,1)S(1)} %fusion.1, s32[32]{0:T(128)S(1)} %reduce), kind=kOutput, calls=%fused_computation.2 | convolution fusion | flops 276828160 | bytes 18874624 | tf_op jit(solution)/shard_map/dot_general | solution.py:41
  155.5 12.4 %copy.19 = bf16[16,8,32,1024]{3,2,1,0:T(8,128)(2,1)} copy(bf16[16,8,32,1024]{3,1,2,0:T(8,128)(2,1)} %bitcast.28) | data formatting | bytes 16777216
  (6 shorter events, 0.0 us)
Async XLA Ops:
  0.6 34.0 %copy-start = (f32[16]{0:T(128)S(1)}, f32[16]{0:T(128)}, u32[]{:S(2)}) copy-start(f32[16]{0:T(128)} %param.6) | copy-start | bytes 196
  2.9 25.9 %all-to-all-start = ((s32[32,1,1]{2,1,0:T(1,128)}), s32[32,1,1]{2,1,0:T(1,128)S(1)}, u32[]{:S(2)}, u32[]{:S(2)}) async-start(s32[32,1,1]{2,1,0:T(1,128)} %copy.13), calls=%async_computation | async-start | bytes 32768 | tf_op jit(solution)/shard_map/all_to_all | solution.py:29
  21.7 13.1 %copy-start.1 = (s32[16,128]{1,0:T(8,128)S(1)}, s32[16,128]{1,0:T(8,128)}, u32[]{:S(2)}) copy-start(s32[16,128]{1,0:T(8,128)} %param.7) | copy-start | bytes 24580
  28.8 116.4 %all-to-all-start.1 = ((bf16[32,1,2,16,1024]{4,3,2,1,0:T(8,128)(2,1)}), bf16[32,1,2,16,1024]{4,3,2,1,0:T(8,128)(2,1)S(1)}, u32[]{:S(2)}, u32[]{:S(2)}) async-start(bf16[32,1,2,16,1024]{4,3,2,1,0:T(8,128)(2,1)} %bitcast.1), calls=%async_computation.1 | async-start | bytes 4194304 | tf_op jit(solution)/shard_map/all_to_all | solution.py:28
where the time goes:
time: 168 us
  blocking collectives  97.7 us (58%)
  local copies, waits for them, and re-layouts  29.7 us (18%)
  other arithmetic  14.2 us (8%)
  matrix products  13.7 us (8%)
  starting transfers between devices  11.8 us (7%)
    unnamed x1, blocking collectives  55.7 us
    psum x1, blocking collectives, on_device(): summed = lax.psum(owner_terms, ('node', 'dev'))  42 us
    unnamed x9, local copies, waits for them, and re-layouts  29 us
    scatter-add x1, other arithmetic, on_device(): jnp.zeros((devices * page_dev,), jnp.float32).at[page_table.reshape(-1)]  11.2 us
    dot_general x1, matrix products, on_device(): jnp.dot(place_sel, arrived.reshape(devices, -1), preferred_element_type=j...  9.09 us
    all_to_all x1, starting transfers between devices, on_device(): lax.all_to_all(dest_local, ('node', 'dev'), split_axis=0, concat_axis=0,...  5.96 us
    all_to_all x1, starting transfers between devices, on_device(): lax.all_to_all(outgoing, ('node', 'dev'), split_axis=0, concat_axis=0, ti...  5.83 us
    dot_general x1, matrix products, on_device(): jnp.dot(pack_sel, flat_pages, preferred_element_type=jnp.float32)  4.61 us
  transfers between devices with their start and end apart: 2, of which 0 were waited for; matrix products, arithmetic and copies ran while one was open for 19% of the time, Pallas kernels for 0%

commit v1 on v0

v1 whole, which is shorter than its diff:
```python
import functools

import jax
import jax.numpy as jnp
from jax import lax
from jax.experimental import pallas as pl
from jax.experimental.pallas import tpu as pltpu
from jax.sharding import PartitionSpec as P


AXES = ("node", "dev")
CHUNKS = 8
SMALL = 1 << 20
WIDE = 58 << 20
EARLY = 2


def quotient(value, size):
    if size & (size - 1) == 0:
        return lax.shift_right_logical(value, size.bit_length() - 1)
    return lax.div(value, size)


def remainder(value, size):
    if size & (size - 1) == 0:
        return lax.bitwise_and(value, size - 1)
    return lax.rem(value, size)


def exchange(x, mask):
    devices = lax.axis_size(AXES)
    return lax.ppermute(x, AXES, [(i, i ^ mask) for i in range(devices)])


def gather_order(devices):
    bits = devices.bit_length() - 1
    early = [1 << (bits - 1 - k) for k in range(EARLY)]
    late = [1 << k for k in range(bits - EARLY)]
    return early, late


def relative(position, masks):
    offset = 0
    for k, mask in enumerate(masks):
        offset = offset + ((position >> k) & 1) * mask
    return offset


def pack_kernel(me_ref, slot_ref, pages_ref, out_ref, page_of, held, in_sems, out_sems):
    devices, page_dev = out_ref.shape[0], pages_ref.shape[0]
    page_of[me_ref[0]] = 0

    def note(page, carry):
        page_of[quotient(slot_ref[page], page_dev)] = page
        return carry

    lax.fori_loop(0, page_dev, note, 0, unroll=16)

    def load(owner):
        return pltpu.make_async_copy(
            pages_ref.at[page_of[owner]], held.at[owner], in_sems.at[owner]
        )

    def store(owner):
        return pltpu.make_async_copy(
            held.at[owner], out_ref.at[owner], out_sems.at[owner]
        )

    def begin(owner, carry):
        load(owner).start()
        return carry

    def turn(owner, carry):
        load(owner).wait()
        store(owner).start()
        return carry

    def end(owner, carry):
        store(owner).wait()
        return carry

    lax.fori_loop(0, devices, begin, 0, unroll=8)
    lax.fori_loop(0, devices, turn, 0, unroll=8)
    lax.fori_loop(0, devices, end, 0, unroll=8)


def keep_kernel(pages_ref, out_ref, held, in_sems, out_sems):
    chunks, rows = held.shape[:2]
    loads = [
        pltpu.make_async_copy(
            pages_ref.at[pl.ds(c * rows, rows)], held.at[c], in_sems.at[c]
        )
        for c in range(chunks)
    ]
    stores = [
        pltpu.make_async_copy(
            held.at[c], out_ref.at[pl.ds(c * rows, rows)], out_sems.at[c]
        )
        for c in range(chunks)
    ]
    for load in loads:
        load.start()
    for load, store in zip(loads, stores):
        load.wait()
        store.start()
    for store in stores:
        store.wait()


def place_kernel(masks, me_ref, slot_ref, arrived_ref, kept_ref, out_ref, sems):
    del kept_ref
    devices = arrived_ref.shape[0]
    me = me_ref[0]
    copies = []
    for position in range(1, devices):
        source = me ^ relative(position, masks)
        copies.append(
            pltpu.make_async_copy(
                arrived_ref.at[source], out_ref.at[slot_ref[position]], sems.at[position]
            )
        )
    for copy in copies:
        copy.start()
    for copy in copies:
        copy.wait()


def heat_kernel(masks, devices, page_dev, me_ref, rate_ref, table_ref, out_ref):
    requests, listed = table_ref.shape
    high_of = relative(lax.broadcasted_iota(jnp.int32, (devices, listed), 0), masks) ^ me_ref[0]
    low_of = lax.broadcasted_iota(jnp.int32, (page_dev, listed), 0)
    total = jnp.zeros((devices, page_dev), jnp.float32)
    for r in range(requests):
        row = table_ref[r : r + 1, :]
        high = (quotient(row, page_dev) == high_of).astype(jnp.float32).astype(jnp.bfloat16)
        low = (remainder(row, page_dev) == low_of).astype(jnp.float32).astype(jnp.bfloat16)
        count = lax.dot_general(
            high, low, (((1,), (1,)), ((), ())), preferred_element_type=jnp.float32
        )
        total = total + rate_ref[r] * count
    out_ref[...] = total


def on_device(kv_pages, new_slot, request_rate, page_table):
    page_dev = kv_pages.shape[0]
    page_shape = kv_pages.shape[1:]
    devices = lax.axis_size(AXES)
    me = lax.axis_index(AXES).astype(jnp.int32)
    smem = pl.BlockSpec(memory_space=pltpu.SMEM)
    vmem = pl.BlockSpec(memory_space=pltpu.VMEM)
    anywhere = pl.BlockSpec(memory_space=pl.ANY)
    chunks = CHUNKS if page_dev % CHUNKS == 0 else 1
    early, late = gather_order(devices)
    masks = early + late

    slots = new_slot[None]
    for mask in early:
        slots = jnp.concatenate([slots, exchange(slots, mask)], axis=0)

    outgoing = pl.pallas_call(
        pack_kernel,
        out_shape=jax.ShapeDtypeStruct((devices,) + page_shape, kv_pages.dtype),
        in_specs=[smem, smem, anywhere],
        out_specs=anywhere,
        scratch_shapes=[
            pltpu.SMEM((devices,), jnp.int32),
            pltpu.VMEM((devices,) + page_shape, kv_pages.dtype),
            pltpu.SemaphoreType.DMA((devices,)),
            pltpu.SemaphoreType.DMA((devices,)),
        ],
        compiler_params=pltpu.CompilerParams(vmem_limit_bytes=WIDE),
        name="pack",
    )(me[None], new_slot, kv_pages)
    arrived = lax.all_to_all(outgoing, AXES, split_axis=0, concat_axis=0, tiled=True)

    heat = pl.pallas_call(
        functools.partial(heat_kernel, masks, devices, page_dev),
        out_shape=jax.ShapeDtypeStruct((devices, page_dev), jnp.float32),
        in_specs=[smem, smem, vmem],
        out_specs=vmem,
        compiler_params=pltpu.CompilerParams(vmem_limit_bytes=4 * SMALL),
        name="heat",
    )(me[None], request_rate, page_table)

    kept = pl.pallas_call(
        keep_kernel,
        out_shape=jax.ShapeDtypeStruct(kv_pages.shape, kv_pages.dtype),
        in_specs=[anywhere],
        out_specs=anywhere,
        scratch_shapes=[
            pltpu.VMEM((chunks, page_dev // chunks) + page_shape, kv_pages.dtype),
            pltpu.SemaphoreType.DMA((chunks,)),
            pltpu.SemaphoreType.DMA((chunks,)),
        ],
        compiler_params=pltpu.CompilerParams(
            vmem_limit_bytes=SMALL + kv_pages.size * kv_pages.dtype.itemsize
        ),
        name="keep",
        cost_estimate=pl.CostEstimate(
            flops=20_000_000_000, bytes_accessed=2 * kv_pages.size * 2, transcendentals=0
        ),
    )(kv_pages)

    for mask in late:
        slots = jnp.concatenate([slots, exchange(slots, mask)], axis=0)
    owners = quotient(slots, page_dev)
    arrived_slot = jnp.sum(jnp.where(owners == me, remainder(slots, page_dev), 0), axis=1)

    targets = jnp.arange(devices, dtype=jnp.int32)
    load = jnp.sum(
        jnp.where(owners[None] == targets[:, None, None], heat[None], 0.0), axis=(1, 2)
    )
    for mask in late:
        load = load + exchange(load, mask)
    offsets = [0]
    for mask in reversed(early):
        offsets = offsets + [o ^ mask for o in offsets]
    terms = [load if o == 0 else exchange(load, o) for o in offsets]
    while len(terms) > 1:
        terms = [a + b for a, b in zip(terms[::2], terms[1::2])]
    device_load = terms[0] / (page_table.shape[1] * page_table.shape[0])

    migrated = pl.pallas_call(
        functools.partial(place_kernel, masks),
        out_shape=jax.ShapeDtypeStruct(kv_pages.shape, kv_pages.dtype),
        in_specs=[smem, smem, anywhere, anywhere],
        out_specs=anywhere,
        scratch_shapes=[pltpu.SemaphoreType.DMA((devices,))],
        input_output_aliases={3: 0},
        compiler_params=pltpu.CompilerParams(vmem_limit_bytes=SMALL),
        name="place",
    )(me[None], arrived_slot, arrived, kept)
    return (migrated, device_load)


def solution(mesh):
    in_specs = (
        P(AXES, None, None, None, None),
        P(AXES),
        P(AXES),
        P(AXES, None),
    )
    out_specs = (P(AXES, None, None, None, None), P())

    return jax.shard_map(
        on_device, mesh=mesh, in_specs=in_specs, out_specs=out_specs, check_vma=False
    )
```

time: 168 us -> 96 us (0.57)
  the two profiles are of different devices: /device:TPU:14 before, /device:TPU:0 now
where the time goes in v1:
time: 96 us; the launch traced here: 95.6 us
  waiting for transfers between devices  59.1 us (62%)
  starting transfers between devices  20.5 us (21%)
  Pallas kernels  10.8 us (11%)
  local copies, waits for them, and re-layouts  3.44 us (4%)
  other arithmetic  0.99 us (1%)
    ppermute x11, waiting for transfers between devices, exchange(): return lax.ppermute(x, AXES, [(i, i ^ mask) for i in range(devices)])  59.1 us
    ppermute x11, starting transfers between devices, exchange(): return lax.ppermute(x, AXES, [(i, i ^ mask) for i in range(devices)])  13.2 us
    all_to_all x1, starting transfers between devices, on_device(): lax.all_to_all(outgoing, AXES, split_axis=0, concat_axis=0, tiled=True)  7.33 us
    pallas_call x1, Pallas kernels, on_device(): pl.pallas_call(keep_kernel, out_shape=jax.ShapeDtypeStruct(kv_pages.shape...  4 us
    pallas_call x1, Pallas kernels, on_device(): pl.pallas_call(pack_kernel, out_shape=jax.ShapeDtypeStruct((devices,) + p...  3.84 us
    unnamed x8, local copies, waits for them, and re-layouts  3.39 us
    pallas_call x1, Pallas kernels, on_device(): pl.pallas_call(functools.partial(place_kernel, masks), out_shape=jax.Shap...  2.09 us
  transfers between devices with their start and end apart: 12, of which 9 were waited for; matrix products, arithmetic and copies ran while one was open for 1% of the time, Pallas kernels for 5%

profile of v1, /device:TPU:0, one launch (start us, length us, event | category | flops | bytes accessed | tf_op | source)
XLA Modules:
  0.0 95.6 jit_solution(10611889490660651154)
XLA Ops:
  0.7 3.8 %pack.1 = bf16[32,1,2,16,1024]{4,3,2,1,0:T(8,128)(2,1)} custom-call(s32[1]{0:T(128)} %bitcast.me_ref, s32[128]{0:T(128)} %slot_ref.1, bf16[128,1,2,16,1024]{4,3,2,1,0:T(8,128)(2,1)} %pages_ref.3), custom_call_target="tpu_custom_call" | custom-call | tf_op jit(solution)/shard_map/pack/pallas_call | solution.py:160
  4.5 7.3 %all-to-all-start = ((bf16[32,1,2,16,1024]{4,3,2,1,0:T(8,128)(2,1)}), bf16[32,1,2,16,1024]{4,3,2,1,0:T(8,128)(2,1)S(1)}, u32[]{:S(2)}, u32[]{:S(2)}) async-start(bf16[32,1,2,16,1024]{4,3,2,1,0:T(8,128)(2,1)} %pack.1), calls=%async_computation | async-start | bytes 4194304 | tf_op jit(solution)/shard_map/all_to_all | solution.py:174
  11.9 2.7 %collective-permute-start = (s32[1,128]{1,0:T(1,128)S(1)}, s32[1,128]{1,0:T(1,128)S(1)}, u32[]{:S(2)}, u32[]{:S(2)}) collective-permute-start(s32[1,128]{1,0:T(1,128)S(1)} %bitcast.2), channel_id=1, source_target_pairs={{0,16},{1,17},{2,18},{3,19},{4,20},{5,21},{6,22},{7,23},{8,24},{9,... | collective-permute-start | bytes 1544 | tf_op jit(solution)/shard_map/ppermute | solution.py:32
  14.6 46.1 %collective-permute-done = s32[1,128]{1,0:T(1,128)S(1)} collective-permute-done((s32[1,128]{1,0:T(1,128)S(1)}, s32[1,128]{1,0:T(1,128)S(1)}, u32[]{:S(2)}, u32[]{:S(2)}) %collective-permute-start) | collective-permute-done | bytes 544 | tf_op jit(solution)/shard_map/ppermute | solution.py:32
  60.7 3.6 %collective-permute-done.1 = s32[2,128]{1,0:T(2,128)S(1)} collective-permute-done((s32[2,128]{1,0:T(2,128)S(1)}, s32[2,128]{1,0:T(2,128)S(1)}, u32[]{:S(2)}, u32[]{:S(2)}) %collective-permute-start.1) | collective-permute-done | bytes 1056 | tf_op jit(solution)/shard_map/ppermute | solution.py:32
  64.3 1.1 %collective-permute-done.2 = s32[4,128]{1,0:T(4,128)S(1)} collective-permute-done((s32[4,128]{1,0:T(4,128)S(1)}, s32[4,128]{1,0:T(4,128)S(1)}, u32[]{:S(2)}, u32[]{:S(2)}) %collective-permute-start.2) | collective-permute-done | bytes 2080 | tf_op jit(solution)/shard_map/ppermute | solution.py:32
  65.5 1.5 %collective-permute-start.3 = (s32[8,128]{1,0:T(8,128)S(1)}, s32[8,128]{1,0:T(8,128)S(1)}, u32[]{:S(2)}, u32[]{:S(2)}) collective-permute-start(s32[8,128]{1,0:T(8,128)S(1)} %pad_add_fusion), channel_id=1, source_target_pairs={{0,2},{1,3},{2,0},{3,1},{4,6},{5,7},{6,4},{7,5},{8,10},{9,11},{10,... | collective-permute-start | bytes 12296 | tf_op jit(solution)/shard_map/ppermute | solution.py:32
  67.0 2.2 %collective-permute-done.3 = s32[8,128]{1,0:T(8,128)S(1)} collective-permute-done((s32[8,128]{1,0:T(8,128)S(1)}, s32[8,128]{1,0:T(8,128)S(1)}, u32[]{:S(2)}, u32[]{:S(2)}) %collective-permute-start.3) | collective-permute-done | bytes 4128 | tf_op jit(solution)/shard_map/ppermute | solution.py:32
  69.2 1.5 %collective-permute-start.4 = (s32[16,128]{1,0:T(8,128)S(1)}, s32[16,128]{1,0:T(8,128)S(1)}, u32[]{:S(2)}, u32[]{:S(2)}) collective-permute-start(s32[16,128]{1,0:T(8,128)S(1)} %concatenate.26), channel_id=1, source_target_pairs={{0,4},{1,5},{2,6},{3,7},{4,0},{5,1},{6,2},{7,3},{8,12},{9,13},{10,... | collective-permute-start | bytes 24584 | tf_op jit(solution)/shard_map/ppermute | solution.py:32
  70.7 0.9 heat.1
  71.6 1.3 %collective-permute-done.4 = s32[16,128]{1,0:T(8,128)S(1)} collective-permute-done((s32[16,128]{1,0:T(8,128)S(1)}, s32[16,128]{1,0:T(8,128)S(1)}, u32[]{:S(2)}, u32[]{:S(2)}) %collective-permute-start.4) | collective-permute-done | bytes 8224 | tf_op jit(solution)/shard_map/ppermute | solution.py:32
  73.0 0.3 select_reduce_fusion
  73.4 1.1 %collective-permute-done.5 = f32[32]{0:T(128)S(1)} collective-permute-done((f32[32]{0:T(128)S(1)}, f32[32]{0:T(128)S(1)}, u32[]{:S(2)}, u32[]{:S(2)}) %collective-permute-start.5) | collective-permute-done | bytes 160 | tf_op jit(solution)/shard_map/ppermute | solution.py:32
  74.6 1.4 %collective-permute-start.6 = (f32[32]{0:T(128)S(1)}, f32[32]{0:T(128)S(1)}, u32[]{:S(2)}, u32[]{:S(2)}) collective-permute-start(f32[32]{0:T(128)S(1)} %add.22), channel_id=1, source_target_pairs={{0,2},{1,3},{2,0},{3,1},{4,6},{5,7},{6,4},{7,5},{8,10},{9,11},{10,... | collective-permute-start | bytes 392 | tf_op jit(solution)/shard_map/ppermute | solution.py:32
  76.0 2.1 %collective-permute-done.6 = f32[32]{0:T(128)S(1)} collective-permute-done((f32[32]{0:T(128)S(1)}, f32[32]{0:T(128)S(1)}, u32[]{:S(2)}, u32[]{:S(2)}) %collective-permute-start.6) | collective-permute-done | bytes 160 | tf_op jit(solution)/shard_map/ppermute | solution.py:32
  78.2 1.4 %collective-permute-start.7 = (f32[32]{0:T(128)S(1)}, f32[32]{0:T(128)S(1)}, u32[]{:S(2)}, u32[]{:S(2)}) collective-permute-start(f32[32]{0:T(128)S(1)} %add.23), channel_id=1, source_target_pairs={{0,4},{1,5},{2,6},{3,7},{4,0},{5,1},{6,2},{7,3},{8,12},{9,13},{10,... | collective-permute-start | bytes 392 | tf_op jit(solution)/shard_map/ppermute | solution.py:32
  79.6 3.4 %copy-done = bf16[128,1,2,16,1024]{4,3,2,1,0:T(8,128)(2,1)S(1)} copy-done((bf16[128,1,2,16,1024]{4,3,2,1,0:T(8,128)(2,1)S(1)}, bf16[128,1,2,16,1024]{4,3,2,1,0:T(8,128)(2,1)}, u32[]{:S(2)}) %copy-start) | copy-done | bytes 8388632
  83.0 4.0 %keep.1.kept_ref = bf16[128,1,2,16,1024]{4,3,2,1,0:T(8,128)(2,1)} custom-call(bf16[128,1,2,16,1024]{4,3,2,1,0:T(8,128)(2,1)S(1)} %copy-done), custom_call_target="tpu_custom_call" | custom-call | flops 20000000000 | bytes 16777216 | tf_op jit(solution)/shard_map/keep/pallas_call | solution.py:185
  87.0 1.5 %collective-permute-start.10 = (f32[32]{0:T(128)S(1)}, f32[32]{0:T(128)S(1)}, u32[]{:S(2)}, u32[]{:S(2)}) collective-permute-start(f32[32]{0:T(128)S(1)} %add.24), channel_id=1, source_target_pairs={{0,24},{1,25},{2,26},{3,27},{4,28},{5,29},{6,30},{7,31},{8,16},{9,... | collective-permute-start | bytes 392 | tf_op jit(solution)/shard_map/ppermute | solution.py:32
  88.5 2.9 %collective-permute-start.8 = (f32[32]{0:T(128)S(1)}, f32[32]{0:T(128)S(1)}, u32[]{:S(2)}, u32[]{:S(2)}) collective-permute-start(f32[32]{0:T(128)S(1)} %add.24), channel_id=1, source_target_pairs={{0,8},{1,9},{2,10},{3,11},{4,12},{5,13},{6,14},{7,15},{8,0},{9,1},... | collective-permute-start | bytes 392 | tf_op jit(solution)/shard_map/ppermute | solution.py:32
  91.4 1.0 %collective-permute-done.10 = f32[32]{0:T(128)S(1)} collective-permute-done((f32[32]{0:T(128)S(1)}, f32[32]{0:T(128)S(1)}, u32[]{:S(2)}, u32[]{:S(2)}) %collective-permute-start.10) | collective-permute-done | bytes 160 | tf_op jit(solution)/shard_map/ppermute | solution.py:32
  92.4 0.6 collective-permute-done.9
  93.0 0.5 add_multiply_fusion
  93.5 2.1 %place.1 = bf16[128,1,2,16,1024]{4,3,2,1,0:T(8,128)(2,1)} custom-call(s32[1]{0:T(128)} %bitcast.me_ref, s32[32]{0:T(128)S(1)} %get-tuple-element.3.slot_ref, bf16[32,1,2,16,1024]{4,3,2,1,0:T(8,128)(2,1)S(1)} %all-to-all-done.arrived_ref, bf16[128,1,2,16,1024]{4,3,2,1,0:T(8,128)(2,1)} %keep.1.kept_ref), custom_call_target="tpu_custom_call", output_to_operand_aliasing={{}: (3, {})} | custom-call | tf_op jit(solution)/shard_map/place/pallas_call | solution.py:223
  (23 shorter events, 0.3 us)
Async XLA Ops:
  0.6 11.2 %copy-start.3 = (s32[128]{0:T(128)S(1)}, s32[128]{0:T(128)}, u32[]{:S(2)}) copy-start(s32[128]{0:T(128)} %slot_ref.1) | copy-start | bytes 1540
  0.6 70.0 %copy-start.1 = (s32[16,128]{1,0:T(8,128)S(1)}, s32[16,128]{1,0:T(8,128)}, u32[]{:S(2)}) copy-start(s32[16,128]{1,0:T(8,128)} %table_ref.1) | copy-start | bytes 24580
  0.7 70.0 %copy-start.2 = (f32[16]{0:T(128)S(1)}, f32[16]{0:T(128)}, u32[]{:S(2)}) copy-start(f32[16]{0:T(128)} %rate_ref.1) | copy-start | bytes 196
  4.5 89.0 %all-to-all-start = ((bf16[32,1,2,16,1024]{4,3,2,1,0:T(8,128)(2,1)}), bf16[32,1,2,16,1024]{4,3,2,1,0:T(8,128)(2,1)S(1)}, u32[]{:S(2)}, u32[]{:S(2)}) async-start(bf16[32,1,2,16,1024]{4,3,2,1,0:T(8,128)(2,1)} %pack.1), calls=%async_computation | async-start | bytes 4194304 | tf_op jit(solution)/shard_map/all_to_all | solution.py:174
  11.9 48.8 %collective-permute-start = (s32[1,128]{1,0:T(1,128)S(1)}, s32[1,128]{1,0:T(1,128)S(1)}, u32[]{:S(2)}, u32[]{:S(2)}) collective-permute-start(s32[1,128]{1,0:T(1,128)S(1)} %bitcast.2), channel_id=1, source_target_pairs={{0,16},{1,17},{2,18},{3,19},{4,20},{5,21},{6,22},{7,23},{8,24},{9,... | collective-permute-start | bytes 1544 | tf_op jit(solution)/shard_map/ppermute | solution.py:32
  60.7 3.6 %collective-permute-start.1 = (s32[2,128]{1,0:T(2,128)S(1)}, s32[2,128]{1,0:T(2,128)S(1)}, u32[]{:S(2)}, u32[]{:S(2)}) collective-permute-start(s32[2,128]{1,0:T(2,128)S(1)} %pad_add_fusion.2), channel_id=1, source_target_pairs={{0,8},{1,9},{2,10},{3,11},{4,12},{5,13},{6,14},{7,15},{8,0},{9,1},... | collective-permute-start | bytes 3080 | tf_op jit(solution)/shard_map/ppermute | solution.py:32
  64.3 1.2 %collective-permute-start.2 = (s32[4,128]{1,0:T(4,128)S(1)}, s32[4,128]{1,0:T(4,128)S(1)}, u32[]{:S(2)}, u32[]{:S(2)}) collective-permute-start(s32[4,128]{1,0:T(4,128)S(1)} %pad_add_fusion.1), channel_id=1, source_target_pairs={{0,1},{1,0},{2,3},{3,2},{4,5},{5,4},{6,7},{7,6},{8,9},{9,8},{10,11... | collective-permute-start | bytes 6152 | tf_op jit(solution)/shard_map/ppermute | solution.py:32
  65.5 3.7 %collective-permute-start.3 = (s32[8,128]{1,0:T(8,128)S(1)}, s32[8,128]{1,0:T(8,128)S(1)}, u32[]{:S(2)}, u32[]{:S(2)}) collective-permute-start(s32[8,128]{1,0:T(8,128)S(1)} %pad_add_fusion), channel_id=1, source_target_pairs={{0,2},{1,3},{2,0},{3,1},{4,6},{5,7},{6,4},{7,5},{8,10},{9,11},{10,... | collective-permute-start | bytes 12296 | tf_op jit(solution)/shard_map/ppermute | solution.py:32
  69.2 3.7 %collective-permute-start.4 = (s32[16,128]{1,0:T(8,128)S(1)}, s32[16,128]{1,0:T(8,128)S(1)}, u32[]{:S(2)}, u32[]{:S(2)}) collective-permute-start(s32[16,128]{1,0:T(8,128)S(1)} %concatenate.26), channel_id=1, source_target_pairs={{0,4},{1,5},{2,6},{3,7},{4,0},{5,1},{6,2},{7,3},{8,12},{9,13},{10,... | collective-permute-start | bytes 24584 | tf_op jit(solution)/shard_map/ppermute | solution.py:32
  73.4 1.2 %collective-permute-start.5 = (f32[32]{0:T(128)S(1)}, f32[32]{0:T(128)S(1)}, u32[]{:S(2)}, u32[]{:S(2)}) collective-permute-start(f32[32]{0:T(128)S(1)} %select_reduce_fusion), channel_id=1, source_target_pairs={{0,1},{1,0},{2,3},{3,2},{4,5},{5,4},{6,7},{7,6},{8,9},{9,8},{10,11... | collective-permute-start | bytes 392 | tf_op jit(solution)/shard_map/ppermute | solution.py:32
  74.6 3.6 %collective-permute-start.6 = (f32[32]{0:T(128)S(1)}, f32[32]{0:T(128)S(1)}, u32[]{:S(2)}, u32[]{:S(2)}) collective-permute-start(f32[32]{0:T(128)S(1)} %add.22), channel_id=1, source_target_pairs={{0,2},{1,3},{2,0},{3,1},{4,6},{5,7},{6,4},{7,5},{8,10},{9,11},{10,... | collective-permute-start | bytes 392 | tf_op jit(solution)/shard_map/ppermute | solution.py:32
  78.2 8.8 %collective-permute-start.7 = (f32[32]{0:T(128)S(1)}, f32[32]{0:T(128)S(1)}, u32[]{:S(2)}, u32[]{:S(2)}) collective-permute-start(f32[32]{0:T(128)S(1)} %add.23), channel_id=1, source_target_pairs={{0,4},{1,5},{2,6},{3,7},{4,0},{5,1},{6,2},{7,3},{8,12},{9,13},{10,... | collective-permute-start | bytes 392 | tf_op jit(solution)/shard_map/ppermute | solution.py:32
  79.6 3.4 %copy-start = (bf16[128,1,2,16,1024]{4,3,2,1,0:T(8,128)(2,1)S(1)}, bf16[128,1,2,16,1024]{4,3,2,1,0:T(8,128)(2,1)}, u32[]{:S(2)}) copy-start(bf16[128,1,2,16,1024]{4,3,2,1,0:T(8,128)(2,1)} %pages_ref.3) | copy-start | bytes 25165828
  87.0 5.4 %collective-permute-start.10 = (f32[32]{0:T(128)S(1)}, f32[32]{0:T(128)S(1)}, u32[]{:S(2)}, u32[]{:S(2)}) collective-permute-start(f32[32]{0:T(128)S(1)} %add.24), channel_id=1, source_target_pairs={{0,24},{1,25},{2,26},{3,27},{4,28},{5,29},{6,30},{7,31},{8,16},{9,... | collective-permute-start | bytes 392 | tf_op jit(solution)/shard_map/ppermute | solution.py:32
  88.5 4.5 %collective-permute-start.9 = (f32[32]{0:T(128)S(1)}, f32[32]{0:T(128)S(1)}, u32[]{:S(2)}, u32[]{:S(2)}) collective-permute-start(f32[32]{0:T(128)S(1)} %add.24), channel_id=1, source_target_pairs={{0,16},{1,17},{2,18},{3,19},{4,20},{5,21},{6,22},{7,23},{8,24},{9,... | collective-permute-start | bytes 392 | tf_op jit(solution)/shard_map/ppermute | solution.py:32
  88.5 4.5 %collective-permute-start.8 = (f32[32]{0:T(128)S(1)}, f32[32]{0:T(128)S(1)}, u32[]{:S(2)}, u32[]{:S(2)}) collective-permute-start(f32[32]{0:T(128)S(1)} %add.24), channel_id=1, source_target_pairs={{0,8},{1,9},{2,10},{3,11},{4,12},{5,13},{6,14},{7,15},{8,0},{9,1},... | collective-permute-start | bytes 392 | tf_op jit(solution)/shard_map/ppermute | solution.py:32

commit v2 on v0

v2 whole, which is shorter than its diff:
```python
import functools

import jax
import jax.numpy as jnp
from jax import lax
from jax.experimental import pallas as pl
from jax.experimental.pallas import tpu as pltpu
from jax.sharding import Mesh, PartitionSpec as P


AXIS = "all"
SMALL = 1 << 20
WIDE = 52 << 20
RELAYED = 2
PARTS = (8,)


def groups(devices):
    parity = lambda d: (d // (devices // 2) + d // 2) % 2
    return [[d for d in range(devices) if parity(d) == p] for p in (0, 1)]


def rank(device):
    return ((device >> 2) << 1) | (device & 1)


def quotient(value, size):
    if size & (size - 1) == 0:
        return lax.shift_right_logical(value, size.bit_length() - 1)
    return lax.div(value, size)


def remainder(value, size):
    if size & (size - 1) == 0:
        return lax.bitwise_and(value, size - 1)
    return lax.rem(value, size)


def exchange(x, mask):
    devices = lax.axis_size(AXIS)
    return lax.ppermute(x, AXIS, [(i, i ^ mask) for i in range(devices)])


def pair_masks(devices):
    half, eighth = devices // 2, devices // 8
    far = sorted((half + 4 * k for k in range(eighth)), key=lambda m: (-(m & 4), m))
    return far + [2 + 4 * k for k in range(eighth)]


def find_pages(slot_ref, page_of, page_dev, me):
    page_of[me] = 0

    def note(page, carry):
        page_of[quotient(slot_ref[page], page_dev)] = page
        return carry

    lax.fori_loop(0, page_dev, note, 0, unroll=16)


def pack_pairs_kernel(far, me_ref, slot_ref, pages_ref, *refs):
    pairs, swap_ref, page_of, sems = refs[:-3], *refs[-3:]
    me = me_ref[0]
    find_pages(slot_ref, page_of, pages_ref.shape[0], me)
    wanted = []
    for k, mask in enumerate(far):
        wanted.append((me ^ mask, pairs[k].at[0]))
        if k < RELAYED:
            wanted.append((me ^ mask ^ 1, pairs[k].at[1]))
        else:
            wanted.append((me ^ mask ^ 1, swap_ref.at[k - RELAYED]))
    copies = [
        pltpu.make_async_copy(pages_ref.at[page_of[owner]], target, sems.at[n])
        for n, (owner, target) in enumerate(wanted)
    ]
    for copy in copies:
        copy.start()
    for copy in copies:
        copy.wait()


def pack_group_kernel(me_ref, slot_ref, pages_ref, group_ref, page_of, held, in_sems, out_sems):
    count, page_dev = group_ref.shape[0], pages_ref.shape[0]
    me = me_ref[0]
    find_pages(slot_ref, page_of, page_dev, me)
    parity = quotient(me, count) ^ (quotient(me, 2) & 1)

    def member(r):
        return (r >> 1 << 2) + (parity ^ int(r >= count // 2)) * 2 + (r & 1)

    loads = [
        pltpu.make_async_copy(pages_ref.at[page_of[member(r)]], held.at[r], in_sems.at[r])
        for r in range(count)
    ]
    stores = [
        pltpu.make_async_copy(held.at[r], group_ref.at[r], out_sems.at[r])
        for r in range(count)
    ]
    for load in loads:
        load.start()
    for load, store in zip(loads, stores):
        load.wait()
        store.start()
    for store in stores:
        store.wait()


def join_kernel(swapped_ref, *refs):
    count = swapped_ref.shape[0]
    outs, sems = refs[count : 2 * count], refs[2 * count]
    copies = [
        pltpu.make_async_copy(swapped_ref.at[k], outs[k].at[1], sems.at[k])
        for k in range(count)
    ]
    for copy in copies:
        copy.start()
    for copy in copies:
        copy.wait()


def keep_kernel(first, rate_ref, table_ref, pages_ref, *refs):
    start, rows = first
    heat_ref = None
    if start:
        _, out_ref, held, in_sems, out_sems = refs
    else:
        out_ref, heat_ref, held, in_sems, out_sems = refs
    chunks = held.shape[0]
    part = lambda c: pl.ds((start + c) * rows, rows)
    loads = [
        pltpu.make_async_copy(pages_ref.at[part(c)], held.at[c], in_sems.at[c])
        for c in range(chunks)
    ]
    stores = [
        pltpu.make_async_copy(held.at[c], out_ref.at[part(c)], out_sems.at[c])
        for c in range(chunks)
    ]
    for load in loads:
        load.start()
    for load, store in zip(loads, stores):
        load.wait()
        store.start()
    if heat_ref is not None:
        heat_ref[...] = page_heat(rate_ref, table_ref, *heat_ref.shape)
    for store in stores:
        store.wait()


def page_heat(rate_ref, table_ref, devices, page_dev):
    requests, listed = table_ref.shape
    high_of = lax.broadcasted_iota(jnp.int32, (devices, listed), 0)
    low_of = lax.broadcasted_iota(jnp.int32, (page_dev, listed), 0)
    total = jnp.zeros((devices, page_dev), jnp.float32)
    for r in range(requests):
        row = table_ref[r : r + 1, :]
        high = (quotient(row, page_dev) == high_of).astype(jnp.float32).astype(jnp.bfloat16)
        low = (remainder(row, page_dev) == low_of).astype(jnp.float32).astype(jnp.bfloat16)
        count = lax.dot_general(
            high, low, (((1,), (1,)), ((), ())), preferred_element_type=jnp.float32
        )
        total = total + rate_ref[r] * count
    return total


def place_kernel(masks, slot_ref, me_ref, *refs):
    *arrived, relayed, group_ref, _, out_ref, sems = refs
    count = group_ref.shape[0]
    me = me_ref[0]
    copies = []

    def place(source, offset):
        slot = slot_ref[me ^ offset]
        copies.append(
            pltpu.make_async_copy(source, out_ref.at[slot], sems.at[len(copies)])
        )

    for k, mask in enumerate(masks):
        place(arrived[k].at[0], mask)
        place(relayed.at[k] if k < RELAYED else arrived[k].at[1], mask ^ 1)
    for offset in groups(2 * count)[0][1:]:
        place(group_ref.at[rank(me ^ offset)], offset)
    for copy in copies:
        copy.start()
    for copy in copies:
        copy.wait()


def on_device(kv_pages, new_slot, request_rate, page_table):
    page_dev = kv_pages.shape[0]
    page_shape = kv_pages.shape[1:]
    dtype = kv_pages.dtype
    devices = lax.axis_size(AXIS)
    me = lax.axis_index(AXIS).astype(jnp.int32)
    smem = pl.BlockSpec(memory_space=pltpu.SMEM)
    vmem = pl.BlockSpec(memory_space=pltpu.VMEM)
    anywhere = pl.BlockSpec(memory_space=pl.ANY)
    masks = pair_masks(devices)
    swaps = len(masks) - RELAYED
    pages = lambda count: jax.ShapeDtypeStruct((count,) + page_shape, dtype)
    wide = pltpu.CompilerParams(vmem_limit_bytes=WIDE)
    small = pltpu.CompilerParams(vmem_limit_bytes=SMALL)

    *pairs, swap = pl.pallas_call(
        functools.partial(pack_pairs_kernel, masks),
        out_shape=[pages(2) for _ in masks] + [pages(swaps)],
        in_specs=[smem, smem, anywhere],
        out_specs=[anywhere] * (len(masks) + 1),
        scratch_shapes=[
            pltpu.SMEM((devices,), jnp.int32),
            pltpu.SemaphoreType.DMA((devices,)),
        ],
        compiler_params=wide,
        name="pack_pairs",
    )(me[None], new_slot, kv_pages)
    swapped = exchange(swap, 1)
    joined = pl.pallas_call(
        join_kernel,
        out_shape=[pages(2)] * swaps,
        in_specs=[anywhere] * (swaps + 1),
        out_specs=[anywhere] * swaps,
        scratch_shapes=[pltpu.SemaphoreType.DMA((swaps,))],
        input_output_aliases={1 + k: k for k in range(swaps)},
        compiler_params=small,
        name="join",
    )(swapped, *pairs[RELAYED:])
    arrived = []
    for mask, pair in zip(masks, pairs[:RELAYED] + list(joined)):
        arrived.append(exchange(pair, mask))
    relayed = exchange(jnp.stack([a[1] for a in arrived[:RELAYED]]), 1)

    slots = lax.all_to_all(
        jnp.broadcast_to(new_slot[None], (devices, page_dev)),
        AXIS, split_axis=0, concat_axis=0, tiled=True,
    )
    owners = quotient(slots, page_dev)
    arrived_slot = jnp.sum(jnp.where(owners == me, remainder(slots, page_dev), 0), axis=1)

    group = pl.pallas_call(
        pack_group_kernel,
        out_shape=pages(devices // 2),
        in_specs=[smem, smem, anywhere],
        out_specs=anywhere,
        scratch_shapes=[
            pltpu.SMEM((devices,), jnp.int32),
            pltpu.VMEM((devices // 2,) + page_shape, dtype),
            pltpu.SemaphoreType.DMA((devices // 2,)),
            pltpu.SemaphoreType.DMA((devices // 2,)),
        ],
        compiler_params=wide,
        name="pack_group",
    )(me[None], new_slot, kv_pages)
    group = lax.all_to_all(
        group, AXIS, split_axis=0, concat_axis=0, tiled=True,
        axis_index_groups=groups(devices),
    )

    rows = page_dev // sum(PARTS)
    start, migrated, heat = 0, [], None
    for n, chunks in enumerate(PARTS):
        *migrated, = pl.pallas_call(
            functools.partial(keep_kernel, (start, rows)),
            out_shape=[jax.ShapeDtypeStruct(kv_pages.shape, dtype)]
            + [jax.ShapeDtypeStruct((devices, page_dev), jnp.float32)] * (n == 0),
            in_specs=[smem, vmem, anywhere] + [anywhere] * (n > 0),
            out_specs=[anywhere] + [vmem] * (n == 0),
            scratch_shapes=[
                pltpu.VMEM((chunks, rows) + page_shape, dtype),
                pltpu.SemaphoreType.DMA((chunks,)),
                pltpu.SemaphoreType.DMA((chunks,)),
            ],
            input_output_aliases={3: 0} if n else {},
            compiler_params=wide,
            cost_estimate=pl.CostEstimate(
                flops=5_000_000_000, bytes_accessed=kv_pages.size, transcendentals=0
            ),
        )(request_rate, page_table, kv_pages, *migrated[:1])
        if n == 0:
            heat = migrated[1]
        start += chunks

    targets = jnp.arange(devices, dtype=jnp.int32)
    load = jnp.sum(
        jnp.where(owners[None] == targets[:, None, None], heat[None], 0.0), axis=(1, 2)
    )
    early, late = sum_masks(devices)
    for mask in late:
        load = load + exchange(load, mask)
    terms = [load]
    for offset in (early[1], early[0], early[0] ^ early[1]):
        terms.append(exchange(load, offset))
    load = (terms[0] + terms[1]) + (terms[2] + terms[3])
    device_load = load / (page_table.shape[1] * page_table.shape[0])

    migrated = pl.pallas_call(
        functools.partial(place_kernel, masks),
        out_shape=jax.ShapeDtypeStruct(kv_pages.shape, dtype),
        in_specs=[smem, smem] + [anywhere] * (len(masks) + 3),
        out_specs=anywhere,
        scratch_shapes=[pltpu.SemaphoreType.DMA((devices,))],
        input_output_aliases={len(masks) + 4: 0},
        compiler_params=small,
        name="place",
    )(arrived_slot, me[None], *arrived, relayed, group, migrated[0])
    return (migrated, device_load)


def sum_masks(devices):
    bits = devices.bit_length() - 1
    return [1 << (bits - 1), 1 << (bits - 2)], [1 << k for k in range(bits - 2)]


def solution(mesh):
    devices = mesh.devices.size
    flat = Mesh(mesh.devices.reshape(devices), (AXIS,))
    in_specs = (
        P(AXIS, None, None, None, None),
        P(AXIS),
        P(AXIS),
        P(AXIS, None),
    )
    out_specs = (P(AXIS, None, None, None, None), P())

    return jax.shard_map(
        on_device, mesh=flat, in_specs=in_specs, out_specs=out_specs, check_vma=False
    )
```

time: 168 us -> 86.3 us (0.51)
  the two profiles are of different devices: /device:TPU:14 before, /device:TPU:0 now
where the time goes in v2:
time: 86.3 us; the launch traced here: 85.9 us
  starting transfers between devices  34.1 us (40%)
  waiting for transfers between devices  33.3 us (39%)
  Pallas kernels  14.8 us (17%)
  local copies, waits for them, and re-layouts  2.01 us (2%)
  other arithmetic  1 us (1%)
    ppermute x16, waiting for transfers between devices, exchange(): return lax.ppermute(x, AXIS, [(i, i ^ mask) for i in range(devices)])  29.7 us
    ppermute x16, starting transfers between devices, exchange(): return lax.ppermute(x, AXIS, [(i, i ^ mask) for i in range(devices)])  23.1 us
    all_to_all x1, starting transfers between devices, on_device(): lax.all_to_all(jnp.broadcast_to(new_slot[None], (devices, page_dev)), AXI...  7.33 us
    pallas_call x1, Pallas kernels, on_device(): pl.pallas_call(functools.partial(keep_kernel, (start, rows)), out_shape=[...  6.97 us
    all_to_all x1, starting transfers between devices, on_device(): lax.all_to_all(group, AXIS, split_axis=0, concat_axis=0, tiled=True, axis...  3.65 us
    all_to_all x1, waiting for transfers between devices, on_device(): lax.all_to_all(jnp.broadcast_to(new_slot[None], (devices, page_dev)), AXI...  3.52 us
    pallas_call x1, Pallas kernels, on_device(): pl.pallas_call(pack_group_kernel, out_shape=pages(devices // 2), in_specs...  2.91 us
    pallas_call x1, Pallas kernels, on_device(): pl.pallas_call(functools.partial(pack_pairs_kernel, masks), out_shape=[pa...  2.27 us
  transfers between devices with their start and end apart: 18, of which 6 were waited for; matrix products, arithmetic and copies ran while one was open for 1% of the time, Pallas kernels for 15%

profile of v2, /device:TPU:0, one launch (start us, length us, event | category | flops | bytes accessed | tf_op | source)
XLA Modules:
  0.0 85.9 jit_solution(163752798647157955)
XLA Ops:
  0.6 1.3 %broadcast_in_dim.30 = s32[32,1,128]{2,1,0:T(1,128)} broadcast(s32[128]{0:T(128)} %slot_ref.3), dimensions={2} | broadcast | bytes 16896 | tf_op jit(solution)/shard_map/broadcast_in_dim | solution.py:231
  2.0 7.3 %all-to-all-start = ((s32[32,1,128]{2,1,0:T(1,128)}), s32[32,1,128]{2,1,0:T(1,128)S(1)}, u32[]{:S(2)}, u32[]{:S(2)}) async-start(s32[32,1,128]{2,1,0:T(1,128)} %broadcast_in_dim.30), calls=%async_computation | async-start | bytes 32768 | tf_op jit(solution)/shard_map/all_to_all | solution.py:230
  9.3 0.6 copy-done
  10.0 2.9 %pack_group.1 = bf16[16,1,2,16,1024]{4,3,2,1,0:T(8,128)(2,1)} custom-call(s32[1]{0:T(128)} %bitcast.3.me_ref, s32[128]{0:T(128)S(1)} %copy-done, bf16[128,1,2,16,1024]{4,3,2,1,0:T(8,128)(2,1)} %pages_ref.5), custom_call_target="tpu_custom_call" | custom-call | tf_op jit(solution)/shard_map/pack_group/pallas_call | solution.py:237
  12.9 3.5 %all-to-all-done = s32[32,1,128]{2,1,0:T(1,128)S(1)} async-done(((s32[32,1,128]{2,1,0:T(1,128)}), s32[32,1,128]{2,1,0:T(1,128)S(1)}, u32[]{:S(2)}, u32[]{:S(2)}) %all-to-all-start) | async-done | bytes 16416 | tf_op jit(solution)/shard_map/all_to_all | solution.py:230
  16.4 3.7 %all-to-all-start.1 = ((bf16[16,1,2,16,1024]{4,3,2,1,0:T(8,128)(2,1)}), bf16[16,1,2,16,1024]{4,3,2,1,0:T(8,128)(2,1)S(1)}, u32[]{:S(2)}, u32[]{:S(2)}) async-start(bf16[16,1,2,16,1024]{4,3,2,1,0:T(8,128)(2,1)} %pack_group.1), calls=%async_computation.1 | async-start | bytes 2097152 | tf_op jit(solution)/shard_map/all_to_all | solution.py:251
  20.1 2.3 %pack_pairs.1 = (bf16[2,1,2,16,1024]{4,3,2,1,0:T(8,128)(2,1)S(1)}, bf16[2,1,2,16,1024]{4,3,2,1,0:T(8,128)(2,1)S(1)}, bf16[2,1,2,16,1024]{4,3,2,1,0:T(8,128)(2,1)...) custom-call(s32[1]{0:T(128)} %bitcast.3.me_ref, ...), custom_call_target="tpu_custom_call" | custom-call | tf_op jit(solution)/shard_map/pack_pairs/pallas_call | solution.py:202
  22.4 3.7 %collective-permute-start = (bf16[2,1,2,16,1024]{4,3,2,1,0:T(8,128)(2,1)S(1)}, bf16[2,1,2,16,1024]{4,3,2,1,0:T(8,128)(2,1)S(1)}, u32[]{:S(2)}, u32[]{:S(2)}) collective-permute-start(bf16[2,1,2,16,1024]{4,3,2,1,0:T(8,128)(2,1)S(1)} %get-tuple-element.19), channel_id=1, source_target_pairs={{0,20},{1,21},{2,22},{3,23},{4,16},{5,17},{6,18},{7,19},{8,28},{9,... | collective-permute-start | bytes 393224 | tf_op jit(solution)/shard_map/ppermute | solution.py:41
  26.1 1.5 %collective-permute-start.1 = (bf16[2,1,2,16,1024]{4,3,2,1,0:T(8,128)(2,1)S(1)}, bf16[2,1,2,16,1024]{4,3,2,1,0:T(8,128)(2,1)S(1)}, u32[]{:S(2)}, u32[]{:S(2)}) collective-permute-start(bf16[2,1,2,16,1024]{4,3,2,1,0:T(8,128)(2,1)S(1)} %get-tuple-element.20), channel_id=1, source_target_pairs={{0,28},{1,29},{2,30},{3,31},{4,24},{5,25},{6,26},{7,27},{8,20},{9,... | collective-permute-start | bytes 393224 | tf_op jit(solution)/shard_map/ppermute | solution.py:41
  27.5 7.0 %shard_map.59 = (bf16[128,1,2,16,1024]{4,3,2,1,0:T(8,128)(2,1)}, f32[32,128]{1,0:T(8,128)S(1)}) custom-call(f32[16]{0:T(128)S(1)} %copy-done.3, s32[16,128]{1,0:T(8,128)S(1)} %copy-done.2, bf16[128,1,2,16,1024]{4,3,2,1,0:T(8,128)(2,1)} %pages_ref.5), custom_call_target="tpu_custom_call" | custom-call | flops 5000000000 | bytes 4194304 | tf_op jit(solution)/shard_map/pallas_call | solution.py:259
  35.4 0.8 collective-permute-done.10
  36.2 1.0 %collective-permute-start.11 = (f32[32]{0:T(128)S(1)}, f32[32]{0:T(128)S(1)}, u32[]{:S(2)}, u32[]{:S(2)}) collective-permute-start(f32[32]{0:T(128)S(1)} %add.18), channel_id=1, source_target_pairs={{0,2},{1,3},{2,0},{3,1},{4,6},{5,7},{6,4},{7,5},{8,10},{9,11},{10,... | collective-permute-start | bytes 392 | tf_op jit(solution)/shard_map/ppermute | solution.py:41
  37.2 19.1 %collective-permute-done.refs_0_ = bf16[2,1,2,16,1024]{4,3,2,1,0:T(8,128)(2,1)S(1)} collective-permute-done((bf16[2,1,2,16,1024]{4,3,2,1,0:T(8,128)(2,1)S(1)}, bf16[2,1,2,16,1024]{4,3,2,1,0:T(8,128)(2,1)S(1)}, u32[]{:S(2)}, u32[]{:S(2)}) %collective-permute-start) | collective-permute-done | bytes 131104 | tf_op jit(solution)/shard_map/ppermute | solution.py:41
  57.1 2.8 %collective-permute-start.3 = (bf16[2,1,2,16,1024]{4,3,2,1,0:T(8,128)(2,1)S(1)}, bf16[2,1,2,16,1024]{4,3,2,1,0:T(8,128)(2,1)S(1)}, u32[]{:S(2)}, u32[]{:S(2)}) collective-permute-start(bf16[2,1,2,16,1024]{4,3,2,1,0:T(8,128)(2,1)S(1)} %get-tuple-element.28), channel_id=1, source_target_pairs={{0,16},{1,17},{2,18},{3,19},{4,20},{5,21},{6,22},{7,23},{8,24},{9,... | collective-permute-start | bytes 393224 | tf_op jit(solution)/shard_map/ppermute | solution.py:41
  60.0 0.8 collective-permute-start.12
  60.9 2.7 %collective-permute-done.12 = f32[32]{0:T(128)S(1)} collective-permute-done((f32[32]{0:T(128)S(1)}, f32[32]{0:T(128)S(1)}, u32[]{:S(2)}, u32[]{:S(2)}) %collective-permute-start.12) | collective-permute-done | bytes 160 | tf_op jit(solution)/shard_map/ppermute | solution.py:41
  63.6 2.4 %collective-permute-start.15 = (f32[32]{0:T(128)S(1)}, f32[32]{0:T(128)S(1)}, u32[]{:S(2)}, u32[]{:S(2)}) collective-permute-start(f32[32]{0:T(128)S(1)} %add.20), channel_id=1, source_target_pairs={{0,24},{1,25},{2,26},{3,27},{4,28},{5,29},{6,30},{7,31},{8,16},{9,... | collective-permute-start | bytes 392 | tf_op jit(solution)/shard_map/ppermute | solution.py:41
  66.0 2.0 %collective-permute-start.13 = (f32[32]{0:T(128)S(1)}, f32[32]{0:T(128)S(1)}, u32[]{:S(2)}, u32[]{:S(2)}) collective-permute-start(f32[32]{0:T(128)S(1)} %add.20), channel_id=1, source_target_pairs={{0,8},{1,9},{2,10},{3,11},{4,12},{5,13},{6,14},{7,15},{8,0},{9,1},... | collective-permute-start | bytes 392 | tf_op jit(solution)/shard_map/ppermute | solution.py:41
  68.0 1.0 %collective-permute-done.15 = f32[32]{0:T(128)S(1)} collective-permute-done((f32[32]{0:T(128)S(1)}, f32[32]{0:T(128)S(1)}, u32[]{:S(2)}, u32[]{:S(2)}) %collective-permute-start.15) | collective-permute-done | bytes 160 | tf_op jit(solution)/shard_map/ppermute | solution.py:41
  69.0 2.4 %collective-permute-start.4 = (bf16[2,1,2,16,1024]{4,3,2,1,0:T(8,128)(2,1)S(1)}, bf16[2,1,2,16,1024]{4,3,2,1,0:T(8,128)(2,1)S(1)}, u32[]{:S(2)}, u32[]{:S(2)}) collective-permute-start(bf16[2,1,2,16,1024]{4,3,2,1,0:T(8,128)(2,1)S(1)} %get-tuple-element.29), channel_id=1, source_target_pairs={{0,24},{1,25},{2,26},{3,27},{4,28},{5,29},{6,30},{7,31},{8,16},{9,... | collective-permute-start | bytes 393224 | tf_op jit(solution)/shard_map/ppermute | solution.py:41
  71.4 1.5 %collective-permute-start.5 = (bf16[2,1,2,16,1024]{4,3,2,1,0:T(8,128)(2,1)S(1)}, bf16[2,1,2,16,1024]{4,3,2,1,0:T(8,128)(2,1)S(1)}, u32[]{:S(2)}, u32[]{:S(2)}) collective-permute-start(bf16[2,1,2,16,1024]{4,3,2,1,0:T(8,128)(2,1)S(1)} %get-tuple-element.30), channel_id=1, source_target_pairs={{0,2},{1,3},{2,0},{3,1},{4,6},{5,7},{6,4},{7,5},{8,10},{9,11},{10,... | collective-permute-start | bytes 393224 | tf_op jit(solution)/shard_map/ppermute | solution.py:41
  73.4 3.8 %collective-permute-start.8 = (bf16[2,1,2,16,1024]{4,3,2,1,0:T(8,128)(2,1)S(1)}, bf16[2,1,2,16,1024]{4,3,2,1,0:T(8,128)(2,1)S(1)}, u32[]{:S(2)}, u32[]{:S(2)}) collective-permute-start(bf16[2,1,2,16,1024]{4,3,2,1,0:T(8,128)(2,1)S(1)} %get-tuple-element.33), channel_id=1, source_target_pairs={{0,14},{1,15},{2,12},{3,13},{4,10},{5,11},{6,8},{7,9},{8,6},{9,7},... | collective-permute-start | bytes 393224 | tf_op jit(solution)/shard_map/ppermute | solution.py:41
  77.7 6.1 %collective-permute-done.5.refs_4_ = bf16[2,1,2,16,1024]{4,3,2,1,0:T(8,128)(2,1)S(1)} collective-permute-done((bf16[2,1,2,16,1024]{4,3,2,1,0:T(8,128)(2,1)S(1)}, bf16[2,1,2,16,1024]{4,3,2,1,0:T(8,128)(2,1)S(1)}, u32[]{:S(2)}, u32[]{:S(2)}) %collective-permute-start.5) | collective-permute-done | bytes 131104 | tf_op jit(solution)/shard_map/ppermute | solution.py:41
  83.8 2.1 %place.1 = bf16[128,1,2,16,1024]{4,3,2,1,0:T(8,128)(2,1)} custom-call(s32[32]{0:T(128)S(1)} %select_reduce_fusion.1.slot_ref, s32[1]{0:T(128)} %bitcast.3.me_ref, bf16[2,1,2,16,1024]{4,3,2,1,0:T(8,128)(2,1)S(1)} %collective-permute-done.refs_0_, bf16[2,1,2,16,1024]{4,3,2,1,0:T(8,128)(2,1)S(1)} %collective-permute-done.1.refs_1_, ...), custom_call_target="tpu_custom_call", output_to_operand_aliasing={{}: (12, {})} | custom-call | tf_op jit(solution)/shard_map/place/pallas_call | solution.py:293
  (37 shorter events, 2.8 us)
Async XLA Ops:
  0.6 19.4 %copy-start.1 = (s32[128]{0:T(128)S(1)}, s32[128]{0:T(128)}, u32[]{:S(2)}) copy-start(s32[128]{0:T(128)} %slot_ref.3) | copy-start | bytes 1540
  2.0 14.4 %all-to-all-start = ((s32[32,1,128]{2,1,0:T(1,128)}), s32[32,1,128]{2,1,0:T(1,128)S(1)}, u32[]{:S(2)}, u32[]{:S(2)}) async-start(s32[32,1,128]{2,1,0:T(1,128)} %broadcast_in_dim.30), calls=%async_computation | async-start | bytes 32768 | tf_op jit(solution)/shard_map/all_to_all | solution.py:230
  9.3 0.7 copy-start
  10.0 17.5 %copy-start.2 = (s32[16,128]{1,0:T(8,128)S(1)}, s32[16,128]{1,0:T(8,128)}, u32[]{:S(2)}) copy-start(s32[16,128]{1,0:T(8,128)} %table_ref.1) | copy-start | bytes 24580
  10.0 17.5 %copy-start.3 = (f32[16]{0:T(128)S(1)}, f32[16]{0:T(128)}, u32[]{:S(2)}) copy-start(f32[16]{0:T(128)} %rate_ref.1) | copy-start | bytes 196
  16.4 67.4 %all-to-all-start.1 = ((bf16[16,1,2,16,1024]{4,3,2,1,0:T(8,128)(2,1)}), bf16[16,1,2,16,1024]{4,3,2,1,0:T(8,128)(2,1)S(1)}, u32[]{:S(2)}, u32[]{:S(2)}) async-start(bf16[16,1,2,16,1024]{4,3,2,1,0:T(8,128)(2,1)} %pack_group.1), calls=%async_computation.1 | async-start | bytes 2097152 | tf_op jit(solution)/shard_map/all_to_all | solution.py:251
  22.4 34.0 %collective-permute-start = (bf16[2,1,2,16,1024]{4,3,2,1,0:T(8,128)(2,1)S(1)}, bf16[2,1,2,16,1024]{4,3,2,1,0:T(8,128)(2,1)S(1)}, u32[]{:S(2)}, u32[]{:S(2)}) collective-permute-start(bf16[2,1,2,16,1024]{4,3,2,1,0:T(8,128)(2,1)S(1)} %get-tuple-element.19), channel_id=1, source_target_pairs={{0,20},{1,21},{2,22},{3,23},{4,16},{5,17},{6,18},{7,19},{8,28},{9,... | collective-permute-start | bytes 393224 | tf_op jit(solution)/shard_map/ppermute | solution.py:41
  26.1 30.3 %collective-permute-start.1 = (bf16[2,1,2,16,1024]{4,3,2,1,0:T(8,128)(2,1)S(1)}, bf16[2,1,2,16,1024]{4,3,2,1,0:T(8,128)(2,1)S(1)}, u32[]{:S(2)}, u32[]{:S(2)}) collective-permute-start(bf16[2,1,2,16,1024]{4,3,2,1,0:T(8,128)(2,1)S(1)} %get-tuple-element.20), channel_id=1, source_target_pairs={{0,28},{1,29},{2,30},{3,31},{4,24},{5,25},{6,26},{7,27},{8,20},{9,... | collective-permute-start | bytes 393224 | tf_op jit(solution)/shard_map/ppermute | solution.py:41
  27.5 29.0 %collective-permute-start.2 = (bf16[6,1,2,16,1024]{4,3,2,1,0:T(8,128)(2,1)S(1)}, bf16[6,1,2,16,1024]{4,3,2,1,0:T(8,128)(2,1)S(1)}, u32[]{:S(2)}, u32[]{:S(2)}) collective-permute-start(bf16[6,1,2,16,1024]{4,3,2,1,0:T(8,128)(2,1)S(1)} %get-tuple-element.21), channel_id=1, source_target_pairs={{0,1},{1,0},{2,3},{3,2},{4,5},{5,4},{6,7},{7,6},{8,9},{9,8},{10,11... | collective-permute-start | bytes 1179656 | tf_op jit(solution)/shard_map/ppermute | solution.py:41
  34.8 1.4 %collective-permute-start.10 = (f32[32]{0:T(128)S(1)}, f32[32]{0:T(128)S(1)}, u32[]{:S(2)}, u32[]{:S(2)}) collective-permute-start(f32[32]{0:T(128)S(1)} %select_reduce_fusion), channel_id=1, source_target_pairs={{0,1},{1,0},{2,3},{3,2},{4,5},{5,4},{6,7},{7,6},{8,9},{9,8},{10,11... | collective-permute-start | bytes 392 | tf_op jit(solution)/shard_map/ppermute | solution.py:41
  36.2 23.8 %collective-permute-start.11 = (f32[32]{0:T(128)S(1)}, f32[32]{0:T(128)S(1)}, u32[]{:S(2)}, u32[]{:S(2)}) collective-permute-start(f32[32]{0:T(128)S(1)} %add.18), channel_id=1, source_target_pairs={{0,2},{1,3},{2,0},{3,1},{4,6},{5,7},{6,4},{7,5},{8,10},{9,11},{10,... | collective-permute-start | bytes 392 | tf_op jit(solution)/shard_map/ppermute | solution.py:41
  56.4 17.0 %collective-permute-start.9 = (bf16[2,1,2,16,1024]{4,3,2,1,0:T(8,128)(2,1)S(1)}, bf16[2,1,2,16,1024]{4,3,2,1,0:T(8,128)(2,1)S(1)}, u32[]{:S(2)}, u32[]{:S(2)}) collective-permute-start(bf16[2,1,2,16,1024]{4,3,2,1,0:T(8,128)(2,1)S(1)} %pad_maximum_fusion), channel_id=1, source_target_pairs={{0,1},{1,0},{2,3},{3,2},{4,5},{5,4},{6,7},{7,6},{8,9},{9,8},{10,11... | collective-permute-start | bytes 393224 | tf_op jit(solution)/shard_map/ppermute | solution.py:41
  57.1 16.3 %collective-permute-start.3 = (bf16[2,1,2,16,1024]{4,3,2,1,0:T(8,128)(2,1)S(1)}, bf16[2,1,2,16,1024]{4,3,2,1,0:T(8,128)(2,1)S(1)}, u32[]{:S(2)}, u32[]{:S(2)}) collective-permute-start(bf16[2,1,2,16,1024]{4,3,2,1,0:T(8,128)(2,1)S(1)} %get-tuple-element.28), channel_id=1, source_target_pairs={{0,16},{1,17},{2,18},{3,19},{4,20},{5,21},{6,22},{7,23},{8,24},{9,... | collective-permute-start | bytes 393224 | tf_op jit(solution)/shard_map/ppermute | solution.py:41
  60.0 3.6 %collective-permute-start.12 = (f32[32]{0:T(128)S(1)}, f32[32]{0:T(128)S(1)}, u32[]{:S(2)}, u32[]{:S(2)}) collective-permute-start(f32[32]{0:T(128)S(1)} %add.19), channel_id=1, source_target_pairs={{0,4},{1,5},{2,6},{3,7},{4,0},{5,1},{6,2},{7,3},{8,12},{9,13},{10,... | collective-permute-start | bytes 392 | tf_op jit(solution)/shard_map/ppermute | solution.py:41
  63.6 5.4 %collective-permute-start.15 = (f32[32]{0:T(128)S(1)}, f32[32]{0:T(128)S(1)}, u32[]{:S(2)}, u32[]{:S(2)}) collective-permute-start(f32[32]{0:T(128)S(1)} %add.20), channel_id=1, source_target_pairs={{0,24},{1,25},{2,26},{3,27},{4,28},{5,29},{6,30},{7,31},{8,16},{9,... | collective-permute-start | bytes 392 | tf_op jit(solution)/shard_map/ppermute | solution.py:41
  66.0 5.4 %collective-permute-start.14 = (f32[32]{0:T(128)S(1)}, f32[32]{0:T(128)S(1)}, u32[]{:S(2)}, u32[]{:S(2)}) collective-permute-start(f32[32]{0:T(128)S(1)} %add.20), channel_id=1, source_target_pairs={{0,16},{1,17},{2,18},{3,19},{4,20},{5,21},{6,22},{7,23},{8,24},{9,... | collective-permute-start | bytes 392 | tf_op jit(solution)/shard_map/ppermute | solution.py:41
  66.0 6.9 %collective-permute-start.13 = (f32[32]{0:T(128)S(1)}, f32[32]{0:T(128)S(1)}, u32[]{:S(2)}, u32[]{:S(2)}) collective-permute-start(f32[32]{0:T(128)S(1)} %add.20), channel_id=1, source_target_pairs={{0,8},{1,9},{2,10},{3,11},{4,12},{5,13},{6,14},{7,15},{8,0},{9,1},... | collective-permute-start | bytes 392 | tf_op jit(solution)/shard_map/ppermute | solution.py:41
  69.0 8.7 %collective-permute-start.4 = (bf16[2,1,2,16,1024]{4,3,2,1,0:T(8,128)(2,1)S(1)}, bf16[2,1,2,16,1024]{4,3,2,1,0:T(8,128)(2,1)S(1)}, u32[]{:S(2)}, u32[]{:S(2)}) collective-permute-start(bf16[2,1,2,16,1024]{4,3,2,1,0:T(8,128)(2,1)S(1)} %get-tuple-element.29), channel_id=1, source_target_pairs={{0,24},{1,25},{2,26},{3,27},{4,28},{5,29},{6,30},{7,31},{8,16},{9,... | collective-permute-start | bytes 393224 | tf_op jit(solution)/shard_map/ppermute | solution.py:41
  71.4 12.4 %collective-permute-start.5 = (bf16[2,1,2,16,1024]{4,3,2,1,0:T(8,128)(2,1)S(1)}, bf16[2,1,2,16,1024]{4,3,2,1,0:T(8,128)(2,1)S(1)}, u32[]{:S(2)}, u32[]{:S(2)}) collective-permute-start(bf16[2,1,2,16,1024]{4,3,2,1,0:T(8,128)(2,1)S(1)} %get-tuple-element.30), channel_id=1, source_target_pairs={{0,2},{1,3},{2,0},{3,1},{4,6},{5,7},{6,4},{7,5},{8,10},{9,11},{10,... | collective-permute-start | bytes 393224 | tf_op jit(solution)/shard_map/ppermute | solution.py:41
  72.9 10.9 %collective-permute-start.6 = (bf16[2,1,2,16,1024]{4,3,2,1,0:T(8,128)(2,1)S(1)}, bf16[2,1,2,16,1024]{4,3,2,1,0:T(8,128)(2,1)S(1)}, u32[]{:S(2)}, u32[]{:S(2)}) collective-permute-start(bf16[2,1,2,16,1024]{4,3,2,1,0:T(8,128)(2,1)S(1)} %get-tuple-element.31), channel_id=1, source_target_pairs={{0,6},{1,7},{2,4},{3,5},{4,2},{5,3},{6,0},{7,1},{8,14},{9,15},{10,... | collective-permute-start | bytes 393224 | tf_op jit(solution)/shard_map/ppermute | solution.py:41
  73.4 10.4 %collective-permute-start.7 = (bf16[2,1,2,16,1024]{4,3,2,1,0:T(8,128)(2,1)S(1)}, bf16[2,1,2,16,1024]{4,3,2,1,0:T(8,128)(2,1)S(1)}, u32[]{:S(2)}, u32[]{:S(2)}) collective-permute-start(bf16[2,1,2,16,1024]{4,3,2,1,0:T(8,128)(2,1)S(1)} %get-tuple-element.32), channel_id=1, source_target_pairs={{0,10},{1,11},{2,8},{3,9},{4,14},{5,15},{6,12},{7,13},{8,2},{9,3},... | collective-permute-start | bytes 393224 | tf_op jit(solution)/shard_map/ppermute | solution.py:41
  73.4 10.4 %collective-permute-start.8 = (bf16[2,1,2,16,1024]{4,3,2,1,0:T(8,128)(2,1)S(1)}, bf16[2,1,2,16,1024]{4,3,2,1,0:T(8,128)(2,1)S(1)}, u32[]{:S(2)}, u32[]{:S(2)}) collective-permute-start(bf16[2,1,2,16,1024]{4,3,2,1,0:T(8,128)(2,1)S(1)} %get-tuple-element.33), channel_id=1, source_target_pairs={{0,14},{1,15},{2,12},{3,13},{4,10},{5,11},{6,8},{7,9},{8,6},{9,7},... | collective-permute-start | bytes 393224 | tf_op jit(solution)/shard_map/ppermute | solution.py:41

commit v3 on v2

--- a/solution.py
+++ b/solution.py
@@ -11,7 +11,7 @@
 AXIS = "all"
 SMALL = 1 << 20
 WIDE = 52 << 20
-RELAYED = 2
+RELAYED = 3
 PARTS = (8,)
 
 
@@ -57,9 +57,13 @@
     lax.fori_loop(0, page_dev, note, 0, unroll=16)
 
 
-def pack_pairs_kernel(far, me_ref, slot_ref, pages_ref, *refs):
-    pairs, swap_ref, page_of, sems = refs[:-3], *refs[-3:]
+def pack_pairs_kernel(far, me_ref, slot_ref, row_ref, pages_ref, *refs):
+    pairs, (swap_ref, rows_ref, page_of, sems, row_sems) = refs[:-5], refs[-5:]
     me = me_ref[0]
+    rows = [
+        pltpu.make_async_copy(row_ref, rows_ref.at[d, 0], row_sems.at[d])
+        for d in range(rows_ref.shape[0])
+    ]
     find_pages(slot_ref, page_of, pages_ref.shape[0], me)
     wanted = []
     for k, mask in enumerate(far):
@@ -72,9 +76,9 @@
         pltpu.make_async_copy(pages_ref.at[page_of[owner]], target, sems.at[n])
         for n, (owner, target) in enumerate(wanted)
     ]
-    for copy in copies:
+    for copy in copies + rows:
         copy.start()
-    for copy in copies:
+    for copy in copies + rows:
         copy.wait()
 
 
@@ -199,18 +203,20 @@
     wide = pltpu.CompilerParams(vmem_limit_bytes=WIDE)
     small = pltpu.CompilerParams(vmem_limit_bytes=SMALL)
 
-    *pairs, swap = pl.pallas_call(
+    *pairs, swap, rows = pl.pallas_call(
         functools.partial(pack_pairs_kernel, masks),
-        out_shape=[pages(2) for _ in masks] + [pages(swaps)],
-        in_specs=[smem, smem, anywhere],
-        out_specs=[anywhere] * (len(masks) + 1),
+        out_shape=[pages(2) for _ in masks]
+        + [pages(swaps), jax.ShapeDtypeStruct((devices, 1, page_dev), jnp.int32)],
+        in_specs=[smem, smem, anywhere, anywhere],
+        out_specs=[anywhere] * (len(masks) + 2),
         scratch_shapes=[
             pltpu.SMEM((devices,), jnp.int32),
+            pltpu.SemaphoreType.DMA((devices,)),
             pltpu.SemaphoreType.DMA((devices,)),
         ],
         compiler_params=wide,
         name="pack_pairs",
-    )(me[None], new_slot, kv_pages)
+    )(me[None], new_slot, new_slot, kv_pages)
     swapped = exchange(swap, 1)
     joined = pl.pallas_call(
         join_kernel,
@@ -227,10 +233,8 @@
         arrived.append(exchange(pair, mask))
     relayed = exchange(jnp.stack([a[1] for a in arrived[:RELAYED]]), 1)
 
-    slots = lax.all_to_all(
-        jnp.broadcast_to(new_slot[None], (devices, page_dev)),
-        AXIS, split_axis=0, concat_axis=0, tiled=True,
-    )
+    slots = lax.all_to_all(rows, AXIS, split_axis=0, concat_axis=0, tiled=True)
+    slots = slots.reshape(devices, page_dev)
     owners = quotient(slots, page_dev)
     arrived_slot = jnp.sum(jnp.where(owners == me, remainder(slots, page_dev), 0), axis=1)
 
@@ -253,17 +257,17 @@
         axis_index_groups=groups(devices),
     )
 
-    rows = page_dev // sum(PARTS)
+    height = page_dev // sum(PARTS)
     start, migrated, heat = 0, [], None
     for n, chunks in enumerate(PARTS):
         *migrated, = pl.pallas_call(
-            functools.partial(keep_kernel, (start, rows)),
+            functools.partial(keep_kernel, (start, height)),
             out_shape=[jax.ShapeDtypeStruct(kv_pages.shape, dtype)]
             + [jax.ShapeDtypeStruct((devices, page_dev), jnp.float32)] * (n == 0),
             in_specs=[smem, vmem, anywhere] + [anywhere] * (n > 0),
             out_specs=[anywhere] + [vmem] * (n == 0),
             scratch_shapes=[
-                pltpu.VMEM((chunks, rows) + page_shape, dtype),
+                pltpu.VMEM((chunks, height) + page_shape, dtype),
                 pltpu.SemaphoreType.DMA((chunks,)),
                 pltpu.SemaphoreType.DMA((chunks,)),
             ],

time: 86.3 us -> 90.3 us (1.046)
  waiting for transfers between devices: 33.3 us -> 39.1 us
  local copies, waits for them, and re-layouts: 2.01 us -> 0.74 us
    ppermute x16, waiting for transfers between devices: 29.7 us -> 35 us  [exchange(): return lax.ppermute(x, AXIS, [(i, i ^ mask) for i in range(devices)])]
    broadcast_in_dim x1 -> x0, local copies, waits for them, and re-layouts: 1.33 us -> none  [on_device(): jnp.broadcast_to(new_slot[None], (devices, page_dev))]
  transfers between devices with their start and end apart: 18 -> 18, of which waited for: 6 -> 7; matrix products, arithmetic and copies ran while one was open for 1% -> 1% of each run, Pallas kernels for 15% -> 11%
where the time goes in v3:
time: 90.3 us; the launch traced here: 89.9 us
  waiting for transfers between devices  39.1 us (43%)
  starting transfers between devices  33.2 us (37%)
  Pallas kernels  15.1 us (17%)
  other arithmetic  1.01 us (1%)
    ppermute x16, waiting for transfers between devices, exchange(): return lax.ppermute(x, AXIS, [(i, i ^ mask) for i in range(devices)])  35 us
    ppermute x16, starting transfers between devices, exchange(): return lax.ppermute(x, AXIS, [(i, i ^ mask) for i in range(devices)])  22.2 us
    all_to_all x1, starting transfers between devices, on_device(): slots = lax.all_to_all(rows, AXIS, split_axis=0, concat_axis=0, tiled=True)  7.33 us
    pallas_call x1, Pallas kernels, on_device(): pl.pallas_call(functools.partial(keep_kernel, (start, height)), out_shape...  6.96 us
    all_to_all x1, waiting for transfers between devices, on_device(): slots = lax.all_to_all(rows, AXIS, split_axis=0, concat_axis=0, tiled=True)  4.17 us
    all_to_all x1, starting transfers between devices, on_device(): lax.all_to_all(group, AXIS, split_axis=0, concat_axis=0, tiled=True, axis...  3.65 us
    pallas_call x1, Pallas kernels, on_device(): pl.pallas_call(pack_group_kernel, out_shape=pages(devices // 2), in_specs...  2.91 us
    pallas_call x1, Pallas kernels, on_device(): pl.pallas_call(functools.partial(pack_pairs_kernel, masks), out_shape=[pa...  2.63 us
  transfers between devices with their start and end apart: 18, of which 7 were waited for; matrix products, arithmetic and copies ran while one was open for 1% of the time, Pallas kernels for 11%

profile of v3, /device:TPU:0, one launch (start us, length us, event | category | flops | bytes accessed | tf_op | source)
XLA Modules:
  0.0 89.9 jit_solution(18348123384451292037)
XLA Ops:
  0.7 0.7 copy-done
  1.4 2.6 %pack_pairs.1 = (bf16[2,1,2,16,1024]{4,3,2,1,0:T(8,128)(2,1)S(1)}, bf16[2,1,2,16,1024]{4,3,2,1,0:T(8,128)(2,1)S(1)}, bf16[2,1,2,16,1024]{4,3,2,1,0:T(8,128)(2,1)...) custom-call(s32[1]{0:T(128)} %bitcast.me_ref, ...), custom_call_target="tpu_custom_call" | custom-call | tf_op jit(solution)/shard_map/pack_pairs/pallas_call | solution.py:206
  4.0 7.3 %all-to-all-start = ((s32[32,1,128]{2,1,0:T(1,128)}), s32[32,1,128]{2,1,0:T(1,128)S(1)}, u32[]{:S(2)}, u32[]{:S(2)}) async-start(s32[32,1,128]{2,1,0:T(1,128)} %get-tuple-element.19), calls=%async_computation | async-start | bytes 32768 | tf_op jit(solution)/shard_map/all_to_all | solution.py:236
  11.4 2.9 %pack_group.1 = bf16[16,1,2,16,1024]{4,3,2,1,0:T(8,128)(2,1)} custom-call(s32[1]{0:T(128)} %bitcast.me_ref, s32[128]{0:T(128)S(1)} %copy-done.1, bf16[128,1,2,16,1024]{4,3,2,1,0:T(8,128)(2,1)} %pages_ref.5), custom_call_target="tpu_custom_call" | custom-call | tf_op jit(solution)/shard_map/pack_group/pallas_call | solution.py:241
  14.3 4.2 %all-to-all-done = s32[32,1,128]{2,1,0:T(1,128)S(1)} async-done(((s32[32,1,128]{2,1,0:T(1,128)}), s32[32,1,128]{2,1,0:T(1,128)S(1)}, u32[]{:S(2)}, u32[]{:S(2)}) %all-to-all-start) | async-done | bytes 16416 | tf_op jit(solution)/shard_map/all_to_all | solution.py:236
  18.4 3.7 %all-to-all-start.1 = ((bf16[16,1,2,16,1024]{4,3,2,1,0:T(8,128)(2,1)}), bf16[16,1,2,16,1024]{4,3,2,1,0:T(8,128)(2,1)S(1)}, u32[]{:S(2)}, u32[]{:S(2)}) async-start(bf16[16,1,2,16,1024]{4,3,2,1,0:T(8,128)(2,1)} %pack_group.1), calls=%async_computation.1 | async-start | bytes 2097152 | tf_op jit(solution)/shard_map/all_to_all | solution.py:255
  22.1 3.6 %collective-permute-start = (bf16[2,1,2,16,1024]{4,3,2,1,0:T(8,128)(2,1)S(1)}, bf16[2,1,2,16,1024]{4,3,2,1,0:T(8,128)(2,1)S(1)}, u32[]{:S(2)}, u32[]{:S(2)}) collective-permute-start(bf16[2,1,2,16,1024]{4,3,2,1,0:T(8,128)(2,1)S(1)} %get-tuple-element.20), channel_id=1, source_target_pairs={{0,20},{1,21},{2,22},{3,23},{4,16},{5,17},{6,18},{7,19},{8,28},{9,... | collective-permute-start | bytes 393224 | tf_op jit(solution)/shard_map/ppermute | solution.py:41
  25.7 1.5 %collective-permute-start.1 = (bf16[2,1,2,16,1024]{4,3,2,1,0:T(8,128)(2,1)S(1)}, bf16[2,1,2,16,1024]{4,3,2,1,0:T(8,128)(2,1)S(1)}, u32[]{:S(2)}, u32[]{:S(2)}) collective-permute-start(bf16[2,1,2,16,1024]{4,3,2,1,0:T(8,128)(2,1)S(1)} %get-tuple-element.21), channel_id=1, source_target_pairs={{0,28},{1,29},{2,30},{3,31},{4,24},{5,25},{6,26},{7,27},{8,20},{9,... | collective-permute-start | bytes 393224 | tf_op jit(solution)/shard_map/ppermute | solution.py:41
  27.2 1.5 %collective-permute-start.2 = (bf16[2,1,2,16,1024]{4,3,2,1,0:T(8,128)(2,1)S(1)}, bf16[2,1,2,16,1024]{4,3,2,1,0:T(8,128)(2,1)S(1)}, u32[]{:S(2)}, u32[]{:S(2)}) collective-permute-start(bf16[2,1,2,16,1024]{4,3,2,1,0:T(8,128)(2,1)S(1)} %get-tuple-element.22), channel_id=1, source_target_pairs={{0,16},{1,17},{2,18},{3,19},{4,20},{5,21},{6,22},{7,23},{8,24},{9,... | collective-permute-start | bytes 393224 | tf_op jit(solution)/shard_map/ppermute | solution.py:41
  28.7 7.0 %shard_map.59 = (bf16[128,1,2,16,1024]{4,3,2,1,0:T(8,128)(2,1)}, f32[32,128]{1,0:T(8,128)S(1)}) custom-call(f32[16]{0:T(128)S(1)} %copy-done.3, s32[16,128]{1,0:T(8,128)S(1)} %copy-done.2, bf16[128,1,2,16,1024]{4,3,2,1,0:T(8,128)(2,1)} %pages_ref.5), custom_call_target="tpu_custom_call" | custom-call | flops 5000000000 | bytes 4194304 | tf_op jit(solution)/shard_map/pallas_call | solution.py:263
  36.5 0.7 collective-permute-done.10
  37.2 1.5 %collective-permute-start.11 = (f32[32]{0:T(128)S(1)}, f32[32]{0:T(128)S(1)}, u32[]{:S(2)}, u32[]{:S(2)}) collective-permute-start(f32[32]{0:T(128)S(1)} %add.18), channel_id=1, source_target_pairs={{0,2},{1,3},{2,0},{3,1},{4,6},{5,7},{6,4},{7,5},{8,10},{9,11},{10,... | collective-permute-start | bytes 392 | tf_op jit(solution)/shard_map/ppermute | solution.py:41
  38.7 22.5 %collective-permute-done.refs_0_ = bf16[2,1,2,16,1024]{4,3,2,1,0:T(8,128)(2,1)S(1)} collective-permute-done((bf16[2,1,2,16,1024]{4,3,2,1,0:T(8,128)(2,1)S(1)}, bf16[2,1,2,16,1024]{4,3,2,1,0:T(8,128)(2,1)S(1)}, u32[]{:S(2)}, u32[]{:S(2)}) %collective-permute-start) | collective-permute-done | bytes 131104 | tf_op jit(solution)/shard_map/ppermute | solution.py:41
  61.3 4.1 %collective-permute-done.2.refs_2_ = bf16[2,1,2,16,1024]{4,3,2,1,0:T(8,128)(2,1)S(1)} collective-permute-done((bf16[2,1,2,16,1024]{4,3,2,1,0:T(8,128)(2,1)S(1)}, bf16[2,1,2,16,1024]{4,3,2,1,0:T(8,128)(2,1)S(1)}, u32[]{:S(2)}, u32[]{:S(2)}) %collective-permute-start.2) | collective-permute-done | bytes 131104 | tf_op jit(solution)/shard_map/ppermute | solution.py:41
  65.5 1.5 %collective-permute-start.12 = (f32[32]{0:T(128)S(1)}, f32[32]{0:T(128)S(1)}, u32[]{:S(2)}, u32[]{:S(2)}) collective-permute-start(f32[32]{0:T(128)S(1)} %add.19), channel_id=1, source_target_pairs={{0,4},{1,5},{2,6},{3,7},{4,0},{5,1},{6,2},{7,3},{8,12},{9,13},{10,... | collective-permute-start | bytes 392 | tf_op jit(solution)/shard_map/ppermute | solution.py:41
  67.2 2.0 %collective-permute-done.12 = f32[32]{0:T(128)S(1)} collective-permute-done((f32[32]{0:T(128)S(1)}, f32[32]{0:T(128)S(1)}, u32[]{:S(2)}, u32[]{:S(2)}) %collective-permute-start.12) | collective-permute-done | bytes 160 | tf_op jit(solution)/shard_map/ppermute | solution.py:41
  69.2 1.7 %collective-permute-start.15 = (f32[32]{0:T(128)S(1)}, f32[32]{0:T(128)S(1)}, u32[]{:S(2)}, u32[]{:S(2)}) collective-permute-start(f32[32]{0:T(128)S(1)} %add.20), channel_id=1, source_target_pairs={{0,24},{1,25},{2,26},{3,27},{4,28},{5,29},{6,30},{7,31},{8,16},{9,... | collective-permute-start | bytes 392 | tf_op jit(solution)/shard_map/ppermute | solution.py:41
  70.8 2.7 %collective-permute-start.13 = (f32[32]{0:T(128)S(1)}, f32[32]{0:T(128)S(1)}, u32[]{:S(2)}, u32[]{:S(2)}) collective-permute-start(f32[32]{0:T(128)S(1)} %add.20), channel_id=1, source_target_pairs={{0,8},{1,9},{2,10},{3,11},{4,12},{5,13},{6,14},{7,15},{8,0},{9,1},... | collective-permute-start | bytes 392 | tf_op jit(solution)/shard_map/ppermute | solution.py:41
  74.0 1.7 %collective-permute-start.4 = (bf16[2,1,2,16,1024]{4,3,2,1,0:T(8,128)(2,1)S(1)}, bf16[2,1,2,16,1024]{4,3,2,1,0:T(8,128)(2,1)S(1)}, u32[]{:S(2)}, u32[]{:S(2)}) collective-permute-start(bf16[2,1,2,16,1024]{4,3,2,1,0:T(8,128)(2,1)S(1)} %get-tuple-element.29), channel_id=1, source_target_pairs={{0,24},{1,25},{2,26},{3,27},{4,28},{5,29},{6,30},{7,31},{8,16},{9,... | collective-permute-start | bytes 393224 | tf_op jit(solution)/shard_map/ppermute | solution.py:41
  75.8 0.5 collective-permute-start.5
  76.3 2.2 %collective-permute-start.6 = (bf16[2,1,2,16,1024]{4,3,2,1,0:T(8,128)(2,1)S(1)}, bf16[2,1,2,16,1024]{4,3,2,1,0:T(8,128)(2,1)S(1)}, u32[]{:S(2)}, u32[]{:S(2)}) collective-permute-start(bf16[2,1,2,16,1024]{4,3,2,1,0:T(8,128)(2,1)S(1)} %get-tuple-element.31), channel_id=1, source_target_pairs={{0,6},{1,7},{2,4},{3,5},{4,2},{5,3},{6,0},{7,1},{8,14},{9,15},{10,... | collective-permute-start | bytes 393224 | tf_op jit(solution)/shard_map/ppermute | solution.py:41
  78.5 3.1 %collective-permute-start.8 = (bf16[2,1,2,16,1024]{4,3,2,1,0:T(8,128)(2,1)S(1)}, bf16[2,1,2,16,1024]{4,3,2,1,0:T(8,128)(2,1)S(1)}, u32[]{:S(2)}, u32[]{:S(2)}) collective-permute-start(bf16[2,1,2,16,1024]{4,3,2,1,0:T(8,128)(2,1)S(1)} %get-tuple-element.33), channel_id=1, source_target_pairs={{0,14},{1,15},{2,12},{3,13},{4,10},{5,11},{6,8},{7,9},{8,6},{9,7},... | collective-permute-start | bytes 393224 | tf_op jit(solution)/shard_map/ppermute | solution.py:41
  82.3 5.5 %collective-permute-done.5.refs_4_ = bf16[2,1,2,16,1024]{4,3,2,1,0:T(8,128)(2,1)S(1)} collective-permute-done((bf16[2,1,2,16,1024]{4,3,2,1,0:T(8,128)(2,1)S(1)}, bf16[2,1,2,16,1024]{4,3,2,1,0:T(8,128)(2,1)S(1)}, u32[]{:S(2)}, u32[]{:S(2)}) %collective-permute-start.5) | collective-permute-done | bytes 131104 | tf_op jit(solution)/shard_map/ppermute | solution.py:41
  87.8 2.1 %place.1 = bf16[128,1,2,16,1024]{4,3,2,1,0:T(8,128)(2,1)} custom-call(s32[32]{0:T(128)S(1)} %select_reduce_fusion.1.slot_ref, s32[1]{0:T(128)} %bitcast.me_ref, bf16[2,1,2,16,1024]{4,3,2,1,0:T(8,128)(2,1)S(1)} %collective-permute-done.refs_0_, bf16[2,1,2,16,1024]{4,3,2,1,0:T(8,128)(2,1)S(1)} %collective-permute-done.1.refs_1_, ...), custom_call_target="tpu_custom_call", output_to_operand_aliasing={{}: (12, {})} | custom-call | tf_op jit(solution)/shard_map/place/pallas_call | solution.py:297
  (37 shorter events, 2.3 us)
Async XLA Ops:
  0.6 10.7 %copy-start.1 = (s32[128]{0:T(128)S(1)}, s32[128]{0:T(128)}, u32[]{:S(2)}) copy-start(s32[128]{0:T(128)} %slot_ref.3) | copy-start | bytes 1540
  0.6 0.7 copy-start
  1.4 27.3 %copy-start.2 = (s32[16,128]{1,0:T(8,128)S(1)}, s32[16,128]{1,0:T(8,128)}, u32[]{:S(2)}) copy-start(s32[16,128]{1,0:T(8,128)} %table_ref.1) | copy-start | bytes 24580
  1.4 27.3 %copy-start.3 = (f32[16]{0:T(128)S(1)}, f32[16]{0:T(128)}, u32[]{:S(2)}) copy-start(f32[16]{0:T(128)} %rate_ref.1) | copy-start | bytes 196
  4.0 14.4 %all-to-all-start = ((s32[32,1,128]{2,1,0:T(1,128)}), s32[32,1,128]{2,1,0:T(1,128)S(1)}, u32[]{:S(2)}, u32[]{:S(2)}) async-start(s32[32,1,128]{2,1,0:T(1,128)} %get-tuple-element.19), calls=%async_computation | async-start | bytes 32768 | tf_op jit(solution)/shard_map/all_to_all | solution.py:236
  18.4 69.4 %all-to-all-start.1 = ((bf16[16,1,2,16,1024]{4,3,2,1,0:T(8,128)(2,1)}), bf16[16,1,2,16,1024]{4,3,2,1,0:T(8,128)(2,1)S(1)}, u32[]{:S(2)}, u32[]{:S(2)}) async-start(bf16[16,1,2,16,1024]{4,3,2,1,0:T(8,128)(2,1)} %pack_group.1), calls=%async_computation.1 | async-start | bytes 2097152 | tf_op jit(solution)/shard_map/all_to_all | solution.py:255
  22.1 39.1 %collective-permute-start = (bf16[2,1,2,16,1024]{4,3,2,1,0:T(8,128)(2,1)S(1)}, bf16[2,1,2,16,1024]{4,3,2,1,0:T(8,128)(2,1)S(1)}, u32[]{:S(2)}, u32[]{:S(2)}) collective-permute-start(bf16[2,1,2,16,1024]{4,3,2,1,0:T(8,128)(2,1)S(1)} %get-tuple-element.20), channel_id=1, source_target_pairs={{0,20},{1,21},{2,22},{3,23},{4,16},{5,17},{6,18},{7,19},{8,28},{9,... | collective-permute-start | bytes 393224 | tf_op jit(solution)/shard_map/ppermute | solution.py:41
  25.7 35.5 %collective-permute-start.1 = (bf16[2,1,2,16,1024]{4,3,2,1,0:T(8,128)(2,1)S(1)}, bf16[2,1,2,16,1024]{4,3,2,1,0:T(8,128)(2,1)S(1)}, u32[]{:S(2)}, u32[]{:S(2)}) collective-permute-start(bf16[2,1,2,16,1024]{4,3,2,1,0:T(8,128)(2,1)S(1)} %get-tuple-element.21), channel_id=1, source_target_pairs={{0,28},{1,29},{2,30},{3,31},{4,24},{5,25},{6,26},{7,27},{8,20},{9,... | collective-permute-start | bytes 393224 | tf_op jit(solution)/shard_map/ppermute | solution.py:41
  27.2 38.2 %collective-permute-start.2 = (bf16[2,1,2,16,1024]{4,3,2,1,0:T(8,128)(2,1)S(1)}, bf16[2,1,2,16,1024]{4,3,2,1,0:T(8,128)(2,1)S(1)}, u32[]{:S(2)}, u32[]{:S(2)}) collective-permute-start(bf16[2,1,2,16,1024]{4,3,2,1,0:T(8,128)(2,1)S(1)} %get-tuple-element.22), channel_id=1, source_target_pairs={{0,16},{1,17},{2,18},{3,19},{4,20},{5,21},{6,22},{7,23},{8,24},{9,... | collective-permute-start | bytes 393224 | tf_op jit(solution)/shard_map/ppermute | solution.py:41
  36.0 1.2 %collective-permute-start.10 = (f32[32]{0:T(128)S(1)}, f32[32]{0:T(128)S(1)}, u32[]{:S(2)}, u32[]{:S(2)}) collective-permute-start(f32[32]{0:T(128)S(1)} %select_reduce_fusion), channel_id=1, source_target_pairs={{0,1},{1,0},{2,3},{3,2},{4,5},{5,4},{6,7},{7,6},{8,9},{9,8},{10,11... | collective-permute-start | bytes 392 | tf_op jit(solution)/shard_map/ppermute | solution.py:41
  36.1 37.5 %collective-permute-start.3 = (bf16[5,1,2,16,1024]{4,3,2,1,0:T(8,128)(2,1)S(1)}, bf16[5,1,2,16,1024]{4,3,2,1,0:T(8,128)(2,1)S(1)}, u32[]{:S(2)}, u32[]{:S(2)}) collective-permute-start(bf16[5,1,2,16,1024]{4,3,2,1,0:T(8,128)(2,1)S(1)} %get-tuple-element.23), channel_id=1, source_target_pairs={{0,1},{1,0},{2,3},{3,2},{4,5},{5,4},{6,7},{7,6},{8,9},{9,8},{10,11... | collective-permute-start | bytes 983048 | tf_op jit(solution)/shard_map/ppermute | solution.py:41
  37.2 28.3 %collective-permute-start.11 = (f32[32]{0:T(128)S(1)}, f32[32]{0:T(128)S(1)}, u32[]{:S(2)}, u32[]{:S(2)}) collective-permute-start(f32[32]{0:T(128)S(1)} %add.18), channel_id=1, source_target_pairs={{0,2},{1,3},{2,0},{3,1},{4,6},{5,7},{6,4},{7,5},{8,10},{9,11},{10,... | collective-permute-start | bytes 392 | tf_op jit(solution)/shard_map/ppermute | solution.py:41
  65.4 13.1 %collective-permute-start.9 = (bf16[3,1,2,16,1024]{4,3,2,1,0:T(8,128)(2,1)S(1)}, bf16[3,1,2,16,1024]{4,3,2,1,0:T(8,128)(2,1)S(1)}, u32[]{:S(2)}, u32[]{:S(2)}) collective-permute-start(bf16[3,1,2,16,1024]{4,3,2,1,0:T(8,128)(2,1)S(1)} %pad_maximum_fusion), channel_id=1, source_target_pairs={{0,1},{1,0},{2,3},{3,2},{4,5},{5,4},{6,7},{7,6},{8,9},{9,8},{10,11... | collective-permute-start | bytes 589832 | tf_op jit(solution)/shard_map/ppermute | solution.py:41
  65.5 3.6 %collective-permute-start.12 = (f32[32]{0:T(128)S(1)}, f32[32]{0:T(128)S(1)}, u32[]{:S(2)}, u32[]{:S(2)}) collective-permute-start(f32[32]{0:T(128)S(1)} %add.19), channel_id=1, source_target_pairs={{0,4},{1,5},{2,6},{3,7},{4,0},{5,1},{6,2},{7,3},{8,12},{9,13},{10,... | collective-permute-start | bytes 392 | tf_op jit(solution)/shard_map/ppermute | solution.py:41
  69.2 6.6 %collective-permute-start.15 = (f32[32]{0:T(128)S(1)}, f32[32]{0:T(128)S(1)}, u32[]{:S(2)}, u32[]{:S(2)}) collective-permute-start(f32[32]{0:T(128)S(1)} %add.20), channel_id=1, source_target_pairs={{0,24},{1,25},{2,26},{3,27},{4,28},{5,29},{6,30},{7,31},{8,16},{9,... | collective-permute-start | bytes 392 | tf_op jit(solution)/shard_map/ppermute | solution.py:41
  70.8 5.5 %collective-permute-start.14 = (f32[32]{0:T(128)S(1)}, f32[32]{0:T(128)S(1)}, u32[]{:S(2)}, u32[]{:S(2)}) collective-permute-start(f32[32]{0:T(128)S(1)} %add.20), channel_id=1, source_target_pairs={{0,16},{1,17},{2,18},{3,19},{4,20},{5,21},{6,22},{7,23},{8,24},{9,... | collective-permute-start | bytes 392 | tf_op jit(solution)/shard_map/ppermute | solution.py:41
  70.8 7.7 %collective-permute-start.13 = (f32[32]{0:T(128)S(1)}, f32[32]{0:T(128)S(1)}, u32[]{:S(2)}, u32[]{:S(2)}) collective-permute-start(f32[32]{0:T(128)S(1)} %add.20), channel_id=1, source_target_pairs={{0,8},{1,9},{2,10},{3,11},{4,12},{5,13},{6,14},{7,15},{8,0},{9,1},... | collective-permute-start | bytes 392 | tf_op jit(solution)/shard_map/ppermute | solution.py:41
  74.0 8.2 %collective-permute-start.4 = (bf16[2,1,2,16,1024]{4,3,2,1,0:T(8,128)(2,1)S(1)}, bf16[2,1,2,16,1024]{4,3,2,1,0:T(8,128)(2,1)S(1)}, u32[]{:S(2)}, u32[]{:S(2)}) collective-permute-start(bf16[2,1,2,16,1024]{4,3,2,1,0:T(8,128)(2,1)S(1)} %get-tuple-element.29), channel_id=1, source_target_pairs={{0,24},{1,25},{2,26},{3,27},{4,28},{5,29},{6,30},{7,31},{8,16},{9,... | collective-permute-start | bytes 393224 | tf_op jit(solution)/shard_map/ppermute | solution.py:41
  75.8 12.1 %collective-permute-start.5 = (bf16[2,1,2,16,1024]{4,3,2,1,0:T(8,128)(2,1)S(1)}, bf16[2,1,2,16,1024]{4,3,2,1,0:T(8,128)(2,1)S(1)}, u32[]{:S(2)}, u32[]{:S(2)}) collective-permute-start(bf16[2,1,2,16,1024]{4,3,2,1,0:T(8,128)(2,1)S(1)} %get-tuple-element.30), channel_id=1, source_target_pairs={{0,2},{1,3},{2,0},{3,1},{4,6},{5,7},{6,4},{7,5},{8,10},{9,11},{10,... | collective-permute-start | bytes 393224 | tf_op jit(solution)/shard_map/ppermute | solution.py:41
  76.3 11.5 %collective-permute-start.6 = (bf16[2,1,2,16,1024]{4,3,2,1,0:T(8,128)(2,1)S(1)}, bf16[2,1,2,16,1024]{4,3,2,1,0:T(8,128)(2,1)S(1)}, u32[]{:S(2)}, u32[]{:S(2)}) collective-permute-start(bf16[2,1,2,16,1024]{4,3,2,1,0:T(8,128)(2,1)S(1)} %get-tuple-element.31), channel_id=1, source_target_pairs={{0,6},{1,7},{2,4},{3,5},{4,2},{5,3},{6,0},{7,1},{8,14},{9,15},{10,... | collective-permute-start | bytes 393224 | tf_op jit(solution)/shard_map/ppermute | solution.py:41
  78.5 9.3 %collective-permute-start.7 = (bf16[2,1,2,16,1024]{4,3,2,1,0:T(8,128)(2,1)S(1)}, bf16[2,1,2,16,1024]{4,3,2,1,0:T(8,128)(2,1)S(1)}, u32[]{:S(2)}, u32[]{:S(2)}) collective-permute-start(bf16[2,1,2,16,1024]{4,3,2,1,0:T(8,128)(2,1)S(1)} %get-tuple-element.32), channel_id=1, source_target_pairs={{0,10},{1,11},{2,8},{3,9},{4,14},{5,15},{6,12},{7,13},{8,2},{9,3},... | collective-permute-start | bytes 393224 | tf_op jit(solution)/shard_map/ppermute | solution.py:41
  78.5 9.3 %collective-permute-start.8 = (bf16[2,1,2,16,1024]{4,3,2,1,0:T(8,128)(2,1)S(1)}, bf16[2,1,2,16,1024]{4,3,2,1,0:T(8,128)(2,1)S(1)}, u32[]{:S(2)}, u32[]{:S(2)}) collective-permute-start(bf16[2,1,2,16,1024]{4,3,2,1,0:T(8,128)(2,1)S(1)} %get-tuple-element.33), channel_id=1, source_target_pairs={{0,14},{1,15},{2,12},{3,13},{4,10},{5,11},{6,8},{7,9},{8,6},{9,7},... | collective-permute-start | bytes 393224 | tf_op jit(solution)/shard_map/ppermute | solution.py:41
